TPU v7x, 256 devices: a whole 4x4x8 slice. The times are simulated.
256 devices in a mesh: planes: 64 (over y, z_hi, x, core), elem: 4 (over z_lo).
Axes of the slice: x: 4, y: 4, z: 8 (z_hi: 2, z_lo: 4; z = z_hi * 4 + z_lo), core: 2. Of those that a mesh axis runs over, the one named last changes fastest.
Arguments:
- velocity: float32 [3, 256, 41472], P(None, 'planes', 'elem'), may hold values from -6 to 6
- geometry: float32 [4, 41472], P(None, 'elem'), may hold values from -1.5 to 1.5
- element_kind: int32 [512], P('elem'), may hold values from 0 to 1
- element_scale: float32 [512], P('elem'), may hold values from 0.5 to 2
- dirichlet: int32 [2, 9, 512], P(None, None, 'elem'), may hold values 0 or 1
- schur_stiffness: float32 [2, 36, 36], replicated, may hold values from -0.2 to 8.5, as said below
- schur_mass: float32 [2, 36, 36], replicated, may hold values from -0.1 to 4.5, as said below
- lift: float32 [2, 36, 81], replicated, may hold values from -0.625 to 0.625
- recover: float32 [2, 81, 36], replicated, may hold values from -1 to 1
Outputs:
- new_velocity: float32 [3, 256, 41472], P(None, 'planes', 'elem')
Inputs may be any that keep to these rules, and one draw needn't show every extreme that they name: `schur_stiffness`: each of the two matrices is symmetric and positive definite. `schur_mass`: each of the two matrices is symmetric and positive definite.
All inputs are finite; a program needn't handle non-finite values. No bound on the sum of `dirichlet` on one device may be relied on, other than what follows from the above.
Results may differ from a plain program's by a relative error of at most 0.0001.
Values sent between devices are 32-bit elements; how exact they have to be, the bound alone decides.
No kernel may reach another device: no remote copies, remote signals or barrier semaphores. Data moves between devices by JAX's collectives and lax.ppermute only.
A program may use at most 128 MiB of HBM per device.

v0:
```python
import functools

import jax
import jax.numpy as jnp
import ml_dtypes
import numpy as np
from jax import lax
from jax.experimental import pallas as pl
from jax.experimental.pallas import tpu as pltpu
from jax.sharding import PartitionSpec as P

PLANES = 256
QUAD = 9
NODE = QUAD * QUAD
GROUPS = 64
PARTS = 4
PART_NODES = 10368
CG_STEPS = 4
BETA_COEF = 0.01
STEP_DT = 0.002
HIGHEST = lax.Precision.HIGHEST
F32 = jnp.float32
BF16 = jnp.bfloat16


def gauss_derivative(points):
    nodes = -np.cos(np.pi * (2 * np.arange(points) + 1) / (2 * points))
    ident = np.eye(points)
    diffs = nodes[:, None] - nodes[None, :] + ident
    weights = 1.0 / np.prod(diffs, axis=1)
    matrix = (weights[None, :] / weights[:, None]) / diffs
    matrix = matrix * (1.0 - ident)
    return matrix - ident * matrix.sum(axis=1)[:, None]


def split_np(table):
    high = table.astype(np.float32).astype(ml_dtypes.bfloat16)
    low = (table - high.astype(np.float64)).astype(np.float32).astype(ml_dtypes.bfloat16)
    return high, low


@functools.lru_cache(None)
def tables():
    z = np.arange(PLANES)
    rows = np.arange(PLANES).reshape(GROUPS, 4).T.reshape(-1)
    waves = (rows + 1) // 2
    angle = 2.0 * np.pi / PLANES * (waves[None, :] * z[:, None] % PLANES)
    cosine, sine = np.cos(angle), np.sin(angle)
    odd = (rows % 2 == 1)[None, :]
    ends = ((rows == 0) | (rows == PLANES - 1))[None, :]
    synth = np.where((rows == 0)[None, :], 1.0, np.where(odd, cosine, sine))
    rate = BETA_COEF * waves[None, :]
    slope = np.where(ends, 0.0, np.where(odd, -rate * sine, rate * cosine))
    weight = np.where(ends[0], 1.0 / PLANES, 2.0 / PLANES)
    analysis = synth.T * weight[:, None]
    deriv = gauss_derivative(QUAD)
    first = np.kron(deriv, np.eye(QUAD))
    second = np.kron(np.eye(QUAD), deriv)
    both = np.zeros((256, 512))
    for c in range(3):
        at = slice(c * NODE, (c + 1) * NODE)
        both[at, c * NODE:(c + 1) * NODE] = first.T
        both[at, 256 + c * NODE:256 + (c + 1) * NODE] = second.T
    out = []
    for table in (np.concatenate([synth, slope], 0), both, analysis):
        out.extend(split_np(table))
    return tuple(out)


@functools.lru_cache(None)
def selections():
    edge = np.zeros((128, 36), np.float32)
    node = np.zeros((256, NODE), np.float32)
    comp_row = np.full(128, -1)
    comp_col = np.full(256, -2)
    for c in range(3):
        for s in range(4):
            for k in range(QUAD):
                edge[s * 32 + c * QUAD + k, s * QUAD + k] = 1
                comp_row[s * 32 + c * QUAD + k] = c
        for n in range(NODE):
            node[c * NODE + n, n] = 1
            comp_col[c * NODE + n] = c
    mask_rn = (comp_row[:, None] == comp_col[None, :]).astype(np.float32)
    mask_rr = ((comp_row[:, None] == comp_row[None, :]) & (comp_row >= 0)[:, None]).astype(np.float32)
    perm = np.zeros((128, 128), np.float32)
    for p in range(GROUPS):
        for el in range(2):
            perm[2 * p + el, el * GROUPS + p] = 1
    spare = [32 * s + 27 + r for s in range(4) for r in range(5)]
    place = np.zeros((128, 24), np.float32)
    for a in range(20):
        place[spare[a], a] = 1
    pick = np.zeros((64, 128), np.float32)
    for c in range(3):
        for k in range(QUAD):
            pick[c * QUAD + k, spare[2 + k]] = 1
            pick[32 + c * QUAD + k, spare[11 + k]] = 1
    return edge, node, mask_rn, mask_rr, perm, place, pick


def split(x):
    high = x.astype(BF16)
    return high, (x - high.astype(F32)).astype(BF16)


def dot3(a, b, dims=(((1,), (0,)), ((), ()))):
    mul = functools.partial(lax.dot_general, dimension_numbers=dims, preferred_element_type=F32)
    return mul(a[0], b[0]) + (mul(a[0], b[1]) + mul(a[1], b[0]))


def dot6(a, b, dims=(((1,), (0,)), ((), ()))):
    return lax.dot_general(a, b, dims, precision=HIGHEST, preferred_element_type=F32)


NT = (((1,), (1,)), ((), ()))


def pack_kernel(v_ref, o_ref):
    lane = lax.broadcasted_iota(jnp.int32, (4, 256), 1)
    for e in range(2 * GROUPS):
        start = NODE * e
        base = min(start // 128 * 128, PART_NODES - 256)
        rows = jnp.zeros((4, 256), F32)
        for c in range(3):
            window = v_ref[c, :, base:base + 256]
            turned = pltpu.roll(window, (NODE * c - (start - base)) % 256, 1)
            rows = jnp.where((lane >= NODE * c) & (lane < NODE * (c + 1)), turned, rows)
        at = 16 * (e // 2) + 4 * (e % 2)
        o_ref[at:at + 4, :] = rows[:, :128]
        o_ref[at + 8:at + 12, :] = rows[:, 128:]


def prep_kernel(at_ref, geo_ref, kind_ref, scale_ref, dir_ref, stiff_ref, mass_ref, lift_ref, rec_ref,
                edge_ref, node_ref, mrn_ref, mrr_ref, perm_ref,
                lift_out, w_out, rec_out, geo_out, aux_out, aux_scr):
    place = at_ref[0]
    lane = lax.broadcasted_iota(jnp.int32, (4, 256), 1)
    for el in range(2):
        start = 2 * NODE * place + NODE * el
        base = pl.multiple_of(jnp.minimum(lax.div(start, 128) * 128, PART_NODES - 256), 128)
        window = geo_ref[:, pl.ds(base, 256)]
        turned = pltpu.roll(window, lax.rem(256 - (start - base), 256), 1)
        tiled = jnp.where(lane < NODE, turned,
                          jnp.where(lane < 2 * NODE, pltpu.roll(turned, NODE, 1), pltpu.roll(turned, 2 * NODE, 1)))
        geo_out[4 * el:4 * el + 4, :] = jnp.where(lane < 3 * NODE, tiled, 0.0)
    wave = lax.div(4 * place + at_ref[1] + 1, 2).astype(F32)
    lam = 1.0 + (BETA_COEF * wave) * (BETA_COEF * wave)
    edge = edge_ref[...]
    node = node_ref[...]
    for t in range(2):
        rows = slice(128 * t, 128 * (t + 1))
        lift_out[rows, :] = dot6(dot6(edge, lift_ref[t]), node, NT) * mrn_ref[...]
        rec_out[rows, :] = dot6(dot6(edge, rec_ref[t], NT), node, NT) * mrn_ref[...]
        mixed = stiff_ref[t] + lam * mass_ref[t]
        w_out[:, rows] = dot6(dot6(edge, mixed), edge, NT) * mrr_ref[...]
    second = (kind_ref[...] == 1).astype(F32)
    aux_scr[...] = jnp.zeros((24, 128), F32)
    aux_scr[0:1, :] = scale_ref[...] * (1.0 - second)
    aux_scr[1:2, :] = scale_ref[...] * second
    aux_scr[2:11, :] = (1 - dir_ref[0]).astype(F32)
    aux_scr[11:20, :] = (1 - dir_ref[1]).astype(F32)
    aux_scr[20:21, :] = second
    aux_out[...] = dot6(aux_scr[...], perm_ref[...])


def advect_kernel(x_ref, th_ref, tl_ref, dh_ref, dl_ref, ah_ref, al_ref, geo_ref, o_ref, items_scr, synth_scr, adv_scr):
    chunk = 64
    lane = lax.broadcasted_iota(jnp.int32, (chunk, 256), 1)
    low = lane < NODE
    mid = lane < 2 * NODE
    for el in range(2):
        for q in range(4):
            for t in range(2):
                items_scr[q * 64:(q + 1) * 64, t * 128:(t + 1) * 128] = x_ref[pl.ds(t * 8 + el * 4 + q, GROUPS, stride=16), :]
        synth_scr[...] = dot3((th_ref[...], tl_ref[...]), split(items_scr[...]))
        geo = geo_ref[4 * el:4 * el + 4, :]
        for at in range(0, 256, chunk):
            values = synth_scr[at:at + chunk, :]
            along_z = synth_scr[256 + at:256 + at + chunk, :]
            both = dot3(split(values), (dh_ref[...], dl_ref[...]))
            along_r = both[:, :256]
            along_s = both[:, 256:]
            along_x = geo[0:1] * along_r + geo[1:2] * along_s
            along_y = geo[2:3] * along_r + geo[3:4] * along_s
            up = pltpu.roll(values, NODE, 1)
            up2 = pltpu.roll(values, 2 * NODE, 1)
            down = pltpu.roll(values, 256 - NODE, 1)
            down2 = pltpu.roll(values, 256 - 2 * NODE, 1)
            u = jnp.where(low, values, jnp.where(mid, up, up2))
            v = jnp.where(low, down, jnp.where(mid, values, up))
            w = jnp.where(low, down2, jnp.where(mid, down, values))
            adv_scr[at:at + chunk, :] = u * along_x + v * along_y + w * along_z
        hat = dot3((ah_ref[...], al_ref[...]), split(adv_scr[...]))
        inter = items_scr[...] - STEP_DT * hat
        for q in range(4):
            for t in range(2):
                o_ref[pl.ds(t * 8 + el * 4 + q, GROUPS, stride=16), :] = inter[q * 64:(q + 1) * 64, t * 128:(t + 1) * 128]


def load_rows(x_ref, q, el, t):
    return x_ref[pl.ds(t * 8 + el * 4 + q, GROUPS, stride=16), :]


def lift_kernel(x_ref, lift_ref, aux_ref, place_ref, o_ref, in_scr):
    for q in range(4):
        for el in range(2):
            at = (2 * q + el) * 64
            for t in range(2):
                in_scr[at:at + 64, t * 128:(t + 1) * 128] = load_rows(x_ref, q, el, t)
    lifted = dot3(split(lift_ref[...]), split(in_scr[...]), NT)
    extra = dot6(place_ref[...], aux_ref[...])
    second = aux_ref[20:21, :] > 0.5
    for q in range(4):
        cols = slice(128 * q, 128 * (q + 1))
        o_ref[q] = jnp.where(second, lifted[128:, cols], lifted[:128, cols]) + extra


def turn(x, shift):
    return pltpu.roll(x, shift % 128, 1)


def cg_kernel(f_ref, w_ref, pick_ref, o_ref):
    lane = lax.broadcasted_iota(jnp.int32, (32, 128), 1)
    p = lane & 63
    el = lane >> 6
    height = 2 * (p & 15) + el
    sub = lax.broadcasted_iota(jnp.int32, (64, 1), 0) & 31
    comp = (sub >= QUAD).astype(jnp.int32) + (sub >= 2 * QUAD).astype(jnp.int32)
    zero = jnp.zeros((32, 128), F32)

    def parts(x):
        return [x[:, 128 * i:128 * (i + 1)] for i in range(PARTS)]

    def right_of(v):
        v = parts(v)
        return jnp.concatenate([jnp.where(p < 48, turn(v[i], -16), turn(v[i + 1], 48) if i < 3 else zero)
                                for i in range(PARTS)], axis=1)

    def from_left(v):
        v = parts(v)
        return jnp.concatenate([jnp.where(p >= 16, turn(v[i], 16), turn(v[i - 1], -48) if i > 0 else zero)
                                for i in range(PARTS)], axis=1)

    def top_of(h):
        return jnp.concatenate([jnp.where(height == 31, 0.0, jnp.where(el == 0, turn(x, 64), turn(x, 63)))
                                for x in parts(h)], axis=1)

    def from_below(h):
        return jnp.concatenate([jnp.where(height == 0, 0.0, jnp.where(el == 1, turn(x, 64), turn(x, -63)))
                                for x in parts(h)], axis=1)

    def vector_of(x):
        v, h = x[:32], x[32:]
        return jnp.concatenate([v, right_of(v), h, top_of(h)], axis=0)

    sent = jnp.concatenate([f_ref[i] for i in range(PARTS)], axis=1)
    free = dot6(pick_ref[...], sent)
    first_scale = sent[27:28]
    second_scale = sent[28:29]
    w = split(w_ref[...])

    def assemble(y):
        return jnp.concatenate([y[:32] + from_left(y[32:64]), y[64:96] + from_below(y[96:])], axis=0) * free

    def total(a, b):
        line = jnp.sum(a * b, axis=1, keepdims=True)
        sums = [jnp.sum(jnp.where(comp == c, line, 0.0), axis=0, keepdims=True) for c in range(3)]
        return jnp.where(comp == 0, sums[0], jnp.where(comp == 1, sums[1], sums[2]))

    residual = assemble(sent)
    direction = residual
    trace = jnp.zeros_like(residual)
    now = total(residual, residual)
    for step in range(CG_STEPS):
        vector = vector_of(direction)
        image = assemble(dot3(w, split(jnp.concatenate([vector * first_scale, vector * second_scale], axis=0))))
        alpha = now / total(direction, image)
        trace = trace + alpha * direction
        if step + 1 < CG_STEPS:
            residual = residual - alpha * image
            fresh = total(residual, residual)
            direction = residual + (fresh / now) * direction
            now = fresh
    vector = vector_of(trace)
    for i in range(PARTS):
        o_ref[i] = vector[:, 128 * i:128 * (i + 1)]


def recover_kernel(at_ref, t_ref, x_ref, rec_ref, aux_ref, o_ref, scr):
    second = aux_ref[20:21, :]
    halves = []
    for q in range(4):
        vector = t_ref[q]
        halves.append(jnp.concatenate([vector * (1.0 - second), vector * second], axis=0))
    stacked = jnp.concatenate(halves, axis=1)
    recovered = dot3(split(stacked.T), split(rec_ref[...]))
    for q in range(4):
        wave = lax.div(4 * at_ref[0] + q + 1, 2).astype(F32)
        lam = 1.0 + (BETA_COEF * wave) * (BETA_COEF * wave)
        weight = 1.0 / jnp.full((64, 128), 1.0 + lam, F32)
        for el in range(2):
            at = (2 * q + el) * 64
            for t in range(2):
                value = load_rows(x_ref, q, el, t) * weight + recovered[at:at + 64, 128 * t:128 * (t + 1)]
                scr[pl.ds(512 * t + 4 * el + q, GROUPS, stride=8), :] = value
    lane = lax.broadcasted_iota(jnp.int32, (4, 128), 1)
    for c in range(3):
        current = jnp.zeros((4, 128), F32)
        for e in range(2 * GROUPS):
            tile, offset = divmod(NODE * e, 128)
            rows = jnp.concatenate([scr[4 * e:4 * e + 4, :], scr[512 + 4 * e:516 + 4 * e, :]], axis=1)
            turned = pltpu.roll(rows, (offset - NODE * c) % 256, 1)
            current = jnp.where(lane >= offset, turned[:, :128], current)
            if offset + NODE >= 128:
                o_ref[c, :, 128 * tile:128 * (tile + 1)] = current
                current = turned[:, 128:]


VMEM = pl.BlockSpec(memory_space=pltpu.VMEM)
SMEM = pl.BlockSpec(memory_space=pltpu.SMEM)


def shape(*dims):
    return jax.ShapeDtypeStruct(dims, F32)


def call(kernel, name, out, args, scalars=0, scratch=()):
    many = isinstance(out, tuple)
    return pl.pallas_call(
        kernel,
        name=name,
        out_shape=out,
        in_specs=[SMEM] * scalars + [VMEM] * (len(args) - scalars),
        out_specs=tuple(VMEM for _ in out) if many else VMEM,
        scratch_shapes=[pltpu.VMEM(dims, F32) for dims in scratch],
    )(*args)


def exchange(value, axis, count):
    return lax.all_to_all(value.reshape(count, -1, 128), axis, split_axis=0, concat_axis=0, tiled=True)


def per_device(velocity, geometry, element_kind, element_scale, dirichlet, schur_stiffness, schur_mass, lift, recover):
    at = jnp.stack([lax.axis_index("planes"), lax.axis_index("elem")]).astype(jnp.int32)
    edge, node, mask_rn, mask_rr, perm, place, pick = selections()
    packed = call(pack_kernel, "pack", shape(1024, 128), (velocity,))
    arrived = exchange(packed, "planes", GROUPS).reshape(1024, 128)
    lift_all, w_all, rec_all, geo, aux = call(
        prep_kernel, "prep",
        (shape(256, 256), shape(128, 256), shape(256, 256), shape(8, 256), shape(24, 128)),
        (at, geometry, element_kind.reshape(1, 128), element_scale.reshape(1, 128), dirichlet,
         schur_stiffness, schur_mass, lift, recover, edge, node, mask_rn, mask_rr, perm),
        scalars=1, scratch=((24, 128),))
    inter = call(advect_kernel, "advect", shape(1024, 128), (arrived,) + tables() + (geo,),
                 scratch=((256, 256), (512, 256), (256, 256)))
    owned = exchange(inter, "planes", GROUPS).reshape(1024, 128)
    lifted = call(lift_kernel, "lift", shape(PARTS, 128, 128), (owned, lift_all, aux, place), scratch=((512, 256),))
    forcing = exchange(lifted, "elem", PARTS)
    traces = call(cg_kernel, "cg", shape(PARTS, 128, 128), (forcing, w_all, pick))
    vectors = exchange(traces, "elem", PARTS)
    return call(recover_kernel, "recover", shape(3, 4, PART_NODES), (at, vectors, owned, rec_all, aux),
                scalars=1, scratch=((1024, 128),))


def solution(mesh):
    in_specs = (
        P(None, "planes", "elem"),
        P(None, "elem"),
        P("elem"),
        P("elem"),
        P(None, None, "elem"),
        P(),
        P(),
        P(),
        P(),
    )
    out_specs = P(None, "planes", "elem")
    return jax.shard_map(per_device, mesh=mesh, in_specs=in_specs, out_specs=out_specs, check_vma=False)
```

profile of v0, /device:TPU:8, one launch (start us, length us, event | category | flops | bytes accessed | tf_op | source)
XLA Modules:
  0.0 103.8 jit_solution(5712619776854807750)
XLA Ops:
  0.0 2.7 %pack.1 = f32[1024,128]{1,0:T(8,128)} custom-call(f32[3,4,10368]{2,1,0:T(4,128)} %v_ref.1), custom_call_target="tpu_custom_call" | custom-call | tf_op jit(solution)/shard_map/pack/pallas_call | solution.py:330
  2.7 14.7 %all-to-all-start = ((f32[64,16,128]{2,1,0:T(8,128)}), f32[64,16,128]{2,1,0:T(8,128)S(1)}, u32[]{:S(2)}, u32[]{:S(2)}) async-start(f32[64,16,128]{2,1,0:T(8,128)} %bitcast.10), calls=%async_computation | async-start | bytes 1048576 | tf_op jit(solution)/shard_map/all_to_all | solution.py:341
  17.4 0.0 copy-start.1
  17.4 0.0 copy-done.5
  17.4 0.6 copy.23.dir_ref
  18.0 0.1 copy-done.1
  18.2 0.6 copy.24.stiff_ref
  18.8 0.2 copy-done.2
  19.0 0.6 copy.25.mass_ref
  19.6 0.1 copy-done.3
  19.7 0.6 copy.26.lift_ref
  20.3 0.1 copy-done.4
  20.5 0.7 copy.27.rec_ref
  21.2 0.6 pad_add_fusion.at_ref
  21.9 3.6 %prep.1 = (f32[256,256]{1,0:T(8,128)}, f32[128,256]{1,0:T(8,128)}, f32[256,256]{1,0:T(8,128)}, f32[8,256]{1,0:T(8,128)}, f32[24,128]{1,0:T(8,128)}) custom-call(s32[2]{0:T(128)} %pad_add_fusion.at_ref, f32[4,10368]{1,0:T(4,128)} %geo_ref.1, s32[1,128]{1,0:T(1,128)} %bitcast.13, f32[1,128]{1,0:T(1,128)} %bitcast.14, s32[2,9,128]{2,1,0:T(8,128)} %copy.23.dir_ref, ...), custom_call_target="tpu_custom_call" | custom-call | tf_op jit(solution)/shard_map/prep/pallas_call | solution.py:330
  25.4 8.6 %all-to-all-done = f32[64,16,128]{2,1,0:T(8,128)S(1)} async-done(((f32[64,16,128]{2,1,0:T(8,128)}), f32[64,16,128]{2,1,0:T(8,128)S(1)}, u32[]{:S(2)}, u32[]{:S(2)}) %all-to-all-start) | async-done | bytes 524320 | tf_op jit(solution)/shard_map/all_to_all | solution.py:341
  34.1 0.8 copy-done
  34.9 4.8 %advect.1 = f32[1024,128]{1,0:T(8,128)} custom-call(f32[1024,128]{1,0:T(8,128)} %bitcast.11, bf16[512,256]{1,0:T(8,128)(2,1)} %constant.40.clone.th_ref, bf16[512,256]{1,0:T(8,128)(2,1)} %constant.41.clone.tl_ref, bf16[256,512]{1,0:T(8,128)(2,1)} %constant.42.clone.dh_ref, bf16[256,512]{1,0:T(8,128)(2,1)} %constant.43.clone.dl_ref, ...), custom_call_target="tpu_custom_call" | custom-call | tf_op jit(solution)/shard_map/advect/pallas_call | solution.py:330
  39.7 21.8 %all_to_all.20 = f32[64,16,128]{2,1,0:T(8,128)} all-to-all(f32[64,16,128]{2,1,0:T(8,128)} %bitcast.12), channel_id=1, replica_groups=mesh['planes'=64,'elem'=4] {'planes'}, dimensions={0} | all-to-all | bytes 1048576 | tf_op jit(solution)/shard_map/all_to_all | solution.py:341
  61.5 2.3 %lift.1 = f32[4,128,128]{2,1,0:T(8,128)} custom-call(f32[1024,128]{1,0:T(8,128)} %bitcast.8, f32[256,256]{1,0:T(8,128)} %get-tuple-element.11.lift_ref, f32[24,128]{1,0:T(8,128)} %get-tuple-element.12.aux_ref, f32[128,24]{1,0:T(8,128)} %constant.46.clone.place_ref), custom_call_target="tpu_custom_call" | custom-call | tf_op jit(solution)/shard_map/lift/pallas_call | solution.py:330
  63.8 19.0 %all_to_all.21.f_ref = f32[4,128,128]{2,1,0:T(8,128)} all-to-all(f32[4,128,128]{2,1,0:T(8,128)} %lift.1), channel_id=1, replica_groups=mesh['planes'=64,'elem'=4] {'elem'}, dimensions={0} | all-to-all | bytes 524288 | tf_op jit(solution)/shard_map/all_to_all | solution.py:341
  82.9 4.8 %cg.1 = f32[4,128,128]{2,1,0:T(8,128)} custom-call(f32[4,128,128]{2,1,0:T(8,128)} %all_to_all.21.f_ref, f32[128,256]{1,0:T(8,128)} %get-tuple-element.13.w_ref, f32[64,128]{1,0:T(8,128)} %constant.47.clone.pick_ref), custom_call_target="tpu_custom_call" | custom-call | tf_op jit(solution)/shard_map/cg/pallas_call | solution.py:330
  87.7 12.7 %all_to_all.22.t_ref = f32[4,128,128]{2,1,0:T(8,128)} all-to-all(f32[4,128,128]{2,1,0:T(8,128)} %cg.1), channel_id=1, replica_groups=mesh['planes'=64,'elem'=4] {'elem'}, dimensions={0} | all-to-all | bytes 524288 | tf_op jit(solution)/shard_map/all_to_all | solution.py:341
  100.4 3.4 %recover.1 = f32[3,4,10368]{2,1,0:T(4,128)} custom-call(s32[2]{0:T(128)} %pad_add_fusion.at_ref, f32[4,128,128]{2,1,0:T(8,128)} %all_to_all.22.t_ref, f32[1024,128]{1,0:T(8,128)} %bitcast.9, f32[256,256]{1,0:T(8,128)} %get-tuple-element.14.rec_ref, f32[24,128]{1,0:T(8,128)} %get-tuple-element.12.aux_ref), custom_call_target="tpu_custom_call" | custom-call | tf_op jit(solution)/shard_map/recover/pallas_call | solution.py:330
  (5 shorter events, 0.0 us)
Async XLA Ops:
  2.7 14.7 %copy-start.5 = (s32[2,9,128]{2,0,1:T(2,128)S(1)}, s32[2,9,128]{2,0,1:T(2,128)}, u32[]{:S(2)}) copy-start(s32[2,9,128]{2,0,1:T(2,128)} %param.26) | copy-start | bytes 27652
  2.7 31.4 %all-to-all-start = ((f32[64,16,128]{2,1,0:T(8,128)}), f32[64,16,128]{2,1,0:T(8,128)S(1)}, u32[]{:S(2)}, u32[]{:S(2)}) async-start(f32[64,16,128]{2,1,0:T(8,128)} %bitcast.10), calls=%async_computation | async-start | bytes 1048576 | tf_op jit(solution)/shard_map/all_to_all | solution.py:341
  17.4 0.8 copy-start.1
  18.2 0.8 copy-start.2
  19.0 0.8 copy-start.3
  19.7 0.8 copy-start.4
  34.1 0.8 copy-start
where the time goes:
time: 105 us; the launch traced here: 104 us
  blocking collectives  53.5 us (51%)
  Pallas kernels  21.6 us (21%)
  starting transfers between devices  14.7 us (14%)
  waiting for transfers between devices  8.65 us (8%)
  local copies, waits for them, and re-layouts  4.6 us (4%)
    all_to_all x3, blocking collectives, exchange(): lax.all_to_all(value.reshape(count, -1, 128), axis, split_axis=0, concat_...  53.5 us
    pallas_call x6, Pallas kernels, call(): pl.pallas_call(kernel, name=name, out_shape=out, in_specs=[SMEM] * scalar...  21.6 us
    all_to_all x1, starting transfers between devices, exchange(): lax.all_to_all(value.reshape(count, -1, 128), axis, split_axis=0, concat_...  14.7 us
    all_to_all x1, waiting for transfers between devices, exchange(): lax.all_to_all(value.reshape(count, -1, 128), axis, split_axis=0, concat_...  8.65 us
    unnamed x17, local copies, waits for them, and re-layouts  4.6 us
  transfers between devices with their start and end apart: 1, of which 1 were waited for; matrix products, arithmetic and copies ran while one was open for 4% of the time, Pallas kernels for 3%

commit v1 on v0

--- a/solution.py
+++ b/solution.py
@@ -202,7 +202,7 @@
     return x_ref[pl.ds(t * 8 + el * 4 + q, GROUPS, stride=16), :]
 
 
-def lift_kernel(x_ref, lift_ref, aux_ref, place_ref, o_ref, in_scr):
+def lift_kernel(at_ref, x_ref, lift_ref, aux_ref, place_ref, o0_ref, o1_ref, o2_ref, o3_ref, in_scr, out_scr):
     for q in range(4):
         for el in range(2):
             at = (2 * q + el) * 64
@@ -213,14 +213,18 @@
     second = aux_ref[20:21, :] > 0.5
     for q in range(4):
         cols = slice(128 * q, 128 * (q + 1))
-        o_ref[q] = jnp.where(second, lifted[128:, cols], lifted[:128, cols]) + extra
+        out_scr[q] = jnp.where(second, lifted[128:, cols], lifted[:128, cols]) + extra
+    for k, ref in enumerate((o0_ref, o1_ref, o2_ref, o3_ref)):
+        ref[...] = out_scr[lax.rem(at_ref[1] + k, PARTS)]
 
 
 def turn(x, shift):
     return pltpu.roll(x, shift % 128, 1)
 
 
-def cg_kernel(f_ref, w_ref, pick_ref, o_ref):
+def cg_kernel(at_ref, f0_ref, f1_ref, f2_ref, f3_ref, w_ref, pick_ref, o0_ref, o1_ref, o2_ref, o3_ref, scr):
+    for k, ref in enumerate((f0_ref, f1_ref, f2_ref, f3_ref)):
+        scr[lax.rem(at_ref[1] + PARTS - k, PARTS)] = ref[...]
     lane = lax.broadcasted_iota(jnp.int32, (32, 128), 1)
     p = lane & 63
     el = lane >> 6
@@ -254,7 +258,7 @@
         v, h = x[:32], x[32:]
         return jnp.concatenate([v, right_of(v), h, top_of(h)], axis=0)
 
-    sent = jnp.concatenate([f_ref[i] for i in range(PARTS)], axis=1)
+    sent = jnp.concatenate([scr[i] for i in range(PARTS)], axis=1)
     free = dot6(pick_ref[...], sent)
     first_scale = sent[27:28]
     second_scale = sent[28:29]
@@ -284,14 +288,18 @@
             now = fresh
     vector = vector_of(trace)
     for i in range(PARTS):
-        o_ref[i] = vector[:, 128 * i:128 * (i + 1)]
-
-
-def recover_kernel(at_ref, t_ref, x_ref, rec_ref, aux_ref, o_ref, scr):
+        scr[i] = vector[:, 128 * i:128 * (i + 1)]
+    for k, ref in enumerate((o0_ref, o1_ref, o2_ref, o3_ref)):
+        ref[...] = scr[lax.rem(at_ref[1] + k, PARTS)]
+
+
+def recover_kernel(at_ref, t0_ref, t1_ref, t2_ref, t3_ref, x_ref, rec_ref, aux_ref, o_ref, scr, t_scr):
+    for k, ref in enumerate((t0_ref, t1_ref, t2_ref, t3_ref)):
+        t_scr[lax.rem(at_ref[1] + PARTS - k, PARTS)] = ref[...]
     second = aux_ref[20:21, :]
     halves = []
     for q in range(4):
-        vector = t_ref[q]
+        vector = t_scr[q]
         halves.append(jnp.concatenate([vector * (1.0 - second), vector * second], axis=0))
     stacked = jnp.concatenate(halves, axis=1)
     recovered = dot3(split(stacked.T), split(rec_ref[...]))
@@ -325,8 +333,12 @@
     return jax.ShapeDtypeStruct(dims, F32)
 
 
-def call(kernel, name, out, args, scalars=0, scratch=()):
+def call(kernel, name, out, args, scalars=0, scratch=(), near=True):
     many = isinstance(out, tuple)
+    args = args[:scalars] + tuple(pltpu.with_memory_space_constraint(jnp.asarray(a), pltpu.VMEM) for a in args[scalars:])
+    if near:
+        outs = tuple(pltpu.VMEM(o.shape, F32) for o in (out if many else (out,)))
+        out = outs if many else outs[0]
     return pl.pallas_call(
         kernel,
         name=name,
@@ -339,6 +351,11 @@
 
 def exchange(value, axis, count):
     return lax.all_to_all(value.reshape(count, -1, 128), axis, split_axis=0, concat_axis=0, tiled=True)
+
+
+def spread(blocks):
+    moved = [lax.ppermute(blocks[k], "elem", [(s, (s + k) % PARTS) for s in range(PARTS)]) for k in range(1, PARTS)]
+    return (blocks[0],) + tuple(moved)
 
 
 def per_device(velocity, geometry, element_kind, element_scale, dirichlet, schur_stiffness, schur_mass, lift, recover):
@@ -355,12 +372,13 @@
     inter = call(advect_kernel, "advect", shape(1024, 128), (arrived,) + tables() + (geo,),
                  scratch=((256, 256), (512, 256), (256, 256)))
     owned = exchange(inter, "planes", GROUPS).reshape(1024, 128)
-    lifted = call(lift_kernel, "lift", shape(PARTS, 128, 128), (owned, lift_all, aux, place), scratch=((512, 256),))
-    forcing = exchange(lifted, "elem", PARTS)
-    traces = call(cg_kernel, "cg", shape(PARTS, 128, 128), (forcing, w_all, pick))
-    vectors = exchange(traces, "elem", PARTS)
-    return call(recover_kernel, "recover", shape(3, 4, PART_NODES), (at, vectors, owned, rec_all, aux),
-                scalars=1, scratch=((1024, 128),))
+    block = shape(128, 128)
+    lifted = call(lift_kernel, "lift", (block,) * PARTS, (at, owned, lift_all, aux, place), scalars=1,
+                  scratch=((512, 256), (PARTS, 128, 128)))
+    traces = call(cg_kernel, "cg", (block,) * PARTS, (at,) + spread(lifted) + (w_all, pick), scalars=1,
+                  scratch=((PARTS, 128, 128),))
+    return call(recover_kernel, "recover", shape(3, 4, PART_NODES), (at,) + spread(traces) + (owned, rec_all, aux),
+                scalars=1, scratch=((1024, 128), (PARTS, 128, 128)), near=False)
 
 
 def solution(mesh):

time: 105 us -> 89.7 us (0.85)
  blocking collectives: 53.5 us -> 21 us
  starting transfers between devices: 14.7 us -> 29.9 us
  waiting for transfers between devices: 8.65 us -> 20.2 us
  Pallas kernels: 21.6 us -> 14.8 us
  local copies, waits for them, and re-layouts: 4.6 us -> 2.12 us
    all_to_all x3 -> x1, blocking collectives: 53.5 us -> 21 us  [exchange(): lax.all_to_all(value.reshape(count, -1, 128), axis, split_axis=0, concat_...]
    ppermute x0 -> x6, starting transfers between devices: none -> 15.1 us  [spread(): lax.ppermute(blocks[k], 'elem', [(s, (s + k) % PARTS) for s in range(PART...]
    ppermute x0 -> x6, waiting for transfers between devices: none -> 7.64 us  [spread(): lax.ppermute(blocks[k], 'elem', [(s, (s + k) % PARTS) for s in range(PART...]
    pallas_call x6, Pallas kernels: 21.6 us -> 14.8 us  [call(): pl.pallas_call(kernel, name=name, out_shape=out, in_specs=[SMEM] * scalar...]
    all_to_all x1, waiting for transfers between devices: 8.65 us -> 12.6 us  [exchange(): lax.all_to_all(value.reshape(count, -1, 128), axis, split_axis=0, concat_...]
    unnamed x17 -> x61, local copies, waits for them, and re-layouts: 4.6 us -> 2.12 us
  transfers between devices with their start and end apart: 1 -> 7, of which waited for: 1 -> 4; matrix products, arithmetic and copies ran while one was open for 4% -> 1% of each run, Pallas kernels for 3% -> 3%
where the time goes in v1:
time: 89.7 us; the launch traced here: 89 us
  starting transfers between devices  29.9 us (33%)
  blocking collectives  21 us (23%)
  waiting for transfers between devices  20.2 us (23%)
  Pallas kernels  14.8 us (16%)
  local copies, waits for them, and re-layouts  2.12 us (2%)
    all_to_all x1, blocking collectives, exchange(): lax.all_to_all(value.reshape(count, -1, 128), axis, split_axis=0, concat_...  21 us
    ppermute x6, starting transfers between devices, spread(): lax.ppermute(blocks[k], 'elem', [(s, (s + k) % PARTS) for s in range(PART...  15.1 us
    pallas_call x6, Pallas kernels, call(): pl.pallas_call(kernel, name=name, out_shape=out, in_specs=[SMEM] * scalar...  14.8 us
    all_to_all x1, starting transfers between devices, exchange(): lax.all_to_all(value.reshape(count, -1, 128), axis, split_axis=0, concat_...  14.7 us
    all_to_all x1, waiting for transfers between devices, exchange(): lax.all_to_all(value.reshape(count, -1, 128), axis, split_axis=0, concat_...  12.6 us
    ppermute x6, waiting for transfers between devices, spread(): lax.ppermute(blocks[k], 'elem', [(s, (s + k) % PARTS) for s in range(PART...  7.64 us
    unnamed x61, local copies, waits for them, and re-layouts  2.12 us
  transfers between devices with their start and end apart: 7, of which 4 were waited for; matrix products, arithmetic and copies ran while one was open for 1% of the time, Pallas kernels for 3%

profile of v1, /device:TPU:8, one launch (start us, length us, event | category | flops | bytes accessed | tf_op | source)
XLA Modules:
  0.0 89.0 jit_solution(9970738987614961856)
XLA Ops:
  0.0 1.0 %copy-done = f32[3,4,10368]{2,1,0:T(4,128)S(1)} copy-done((f32[3,4,10368]{2,1,0:T(4,128)S(1)}, f32[3,4,10368]{2,1,0:T(4,128)}, u32[]{:S(2)}) %copy-start) | copy-done | bytes 497688
  1.0 1.7 %pack.1 = f32[1024,128]{1,0:T(8,128)} custom-call(f32[3,4,10368]{2,1,0:T(4,128)S(1)} %copy-done), custom_call_target="tpu_custom_call" | custom-call | tf_op jit(solution)/shard_map/pack/pallas_call | solution.py:342
  2.7 0.0 copy-start.12
  2.8 14.7 %all-to-all-start = ((f32[64,16,128]{2,1,0:T(8,128)}), f32[64,16,128]{2,1,0:T(8,128)S(1)}, u32[]{:S(2)}, u32[]{:S(2)}) async-start(f32[64,16,128]{2,1,0:T(8,128)} %bitcast.2), calls=%async_computation | async-start | bytes 1048576 | tf_op jit(solution)/shard_map/all_to_all | solution.py:353
  17.6 0.7 copy-done.23
  18.4 0.1 copy.27.rec_ref
  18.5 0.6 pad_add_fusion.at_ref
  19.1 0.1 copy-done.9
  19.2 2.3 %prep.1 = (f32[256,256]{1,0:T(8,128)S(1)}, f32[128,256]{1,0:T(8,128)S(1)}, f32[256,256]{1,0:T(8,128)S(1)}, f32[8,256]{1,0:T(8,128)S(1)}, f32[24,128]{1,0:T(8,128)S(1)}) custom-call(s32[2]{0:T(128)} %pad_add_fusion.at_ref, f32[4,10368]{1,0:T(4,128)S(1)} %copy-done.9, s32[1,128]{1,0:T(1,128)S(1)} %bitcast.12, f32[1,128]{1,0:T(1,128)S(1)} %bitcast.13, ...), custom_call_target="tpu_custom_call" | custom-call | tf_op jit(solution)/shard_map/prep/pallas_call | solution.py:342
  21.6 12.6 %all-to-all-done = f32[64,16,128]{2,1,0:T(8,128)S(1)} async-done(((f32[64,16,128]{2,1,0:T(8,128)}), f32[64,16,128]{2,1,0:T(8,128)S(1)}, u32[]{:S(2)}, u32[]{:S(2)}) %all-to-all-start) | async-done | bytes 524320 | tf_op jit(solution)/shard_map/all_to_all | solution.py:353
  34.2 2.6 %advect.1 = f32[1024,128]{1,0:T(8,128)S(1)} custom-call(f32[1024,128]{1,0:T(8,128)S(1)} %bitcast.10, bf16[512,256]{1,0:T(8,128)(2,1)S(1)} %copy-done.1, bf16[512,256]{1,0:T(8,128)(2,1)S(1)} %copy-done.2, bf16[256,512]{1,0:T(8,128)(2,1)S(1)} %copy-done.3, bf16[256,512]{1,0:T(8,128)(2,1)S(1)} %copy-done.4, bf16[256,256]{1,0:T(8,128)(2,1)S(1)} %copy-done.10, ...), custom_call_target="tpu_custom_call" | custom-call | tf_op jit(solution)/shard_map/advect/pallas_call | solution.py:342
  36.9 21.0 %all_to_all.10 = f32[64,16,128]{2,1,0:T(8,128)S(1)} all-to-all(f32[64,16,128]{2,1,0:T(8,128)S(1)} %bitcast.11), channel_id=1, replica_groups=mesh['planes'=64,'elem'=4] {'planes'}, dimensions={0} | all-to-all | bytes 1048576 | tf_op jit(solution)/shard_map/all_to_all | solution.py:353
  57.9 1.4 %lift.1 = (f32[128,128]{1,0:T(8,128)S(1)}, f32[128,128]{1,0:T(8,128)S(1)}, f32[128,128]{1,0:T(8,128)S(1)}, f32[128,128]{1,0:T(8,128)S(1)}) custom-call(s32[2]{0:T(128)} %pad_add_fusion.at_ref, f32[1024,128]{1,0:T(8,128)S(1)} %bitcast.8, f32[256,256]{1,0:T(8,128)S(1)} %copy-done.6, f32[24,128]{1,0:T(8,128)S(1)} %get-tuple-element.20.aux_ref, ...), custom_call_target="tpu_custom_call" | custom-call | tf_op jit(solution)/shard_map/lift/pallas_call | solution.py:342
  59.3 7.9 %collective-permute-start = (f32[128,128]{1,0:T(8,128)S(1)}, f32[128,128]{1,0:T(8,128)S(1)}, u32[]{:S(2)}, u32[]{:S(2)}) collective-permute-start(f32[128,128]{1,0:T(8,128)S(1)} %get-tuple-element.22), channel_id=1, source_target_pairs={{0,1},{1,2},{2,3},{3,0},{4,5},{5,6},{6,7},{7,4},{8,9},{9,10},{10,1... | collective-permute-start | bytes 196616 | tf_op jit(solution)/shard_map/ppermute | solution.py:357
  67.2 0.4 collective-permute-start.1
  67.7 2.8 %collective-permute-start.2 = (f32[128,128]{1,0:T(8,128)S(1)}, f32[128,128]{1,0:T(8,128)S(1)}, u32[]{:S(2)}, u32[]{:S(2)}) collective-permute-start(f32[128,128]{1,0:T(8,128)S(1)} %get-tuple-element.24), channel_id=1, source_target_pairs={{0,3},{1,0},{2,1},{3,2},{4,7},{5,4},{6,5},{7,6},{8,11},{9,8},{10,9... | collective-permute-start | bytes 196616 | tf_op jit(solution)/shard_map/ppermute | solution.py:357
  70.5 3.3 %collective-permute-done.1.f2_ref = f32[128,128]{1,0:T(8,128)S(1)} collective-permute-done((f32[128,128]{1,0:T(8,128)S(1)}, f32[128,128]{1,0:T(8,128)S(1)}, u32[]{:S(2)}, u32[]{:S(2)}) %collective-permute-start.1) | collective-permute-done | bytes 65568 | tf_op jit(solution)/shard_map/ppermute | solution.py:357
  73.8 3.9 %cg.1 = (f32[128,128]{1,0:T(8,128)S(1)}, f32[128,128]{1,0:T(8,128)S(1)}, f32[128,128]{1,0:T(8,128)S(1)}, f32[128,128]{1,0:T(8,128)S(1)}) custom-call(s32[2]{0:T(128)} %pad_add_fusion.at_ref, f32[128,128]{1,0:T(8,128)S(1)} %get-tuple-element.21.f0_ref, f32[128,128]{1,0:T(8,128)S(1)} %collective-permute-done.f1_ref, ...), custom_call_target="tpu_custom_call" | custom-call | tf_op jit(solution)/shard_map/cg/pallas_call | solution.py:342
  77.8 1.5 %collective-permute-start.3 = (f32[128,128]{1,0:T(8,128)S(1)}, f32[128,128]{1,0:T(8,128)S(1)}, u32[]{:S(2)}, u32[]{:S(2)}) collective-permute-start(f32[128,128]{1,0:T(8,128)S(1)} %get-tuple-element.27), channel_id=1, source_target_pairs={{0,1},{1,2},{2,3},{3,0},{4,5},{5,6},{6,7},{7,4},{8,9},{9,10},{10,1... | collective-permute-start | bytes 196616 | tf_op jit(solution)/shard_map/ppermute | solution.py:357
  79.3 2.1 %collective-permute-start.4 = (f32[128,128]{1,0:T(8,128)S(1)}, f32[128,128]{1,0:T(8,128)S(1)}, u32[]{:S(2)}, u32[]{:S(2)}) collective-permute-start(f32[128,128]{1,0:T(8,128)S(1)} %get-tuple-element.28), channel_id=1, source_target_pairs={{0,2},{1,3},{2,0},{3,1},{4,6},{5,7},{6,4},{7,5},{8,10},{9,11},{10,... | collective-permute-start | bytes 196616 | tf_op jit(solution)/shard_map/ppermute | solution.py:357
  81.3 0.4 collective-permute-start.5
  81.7 2.9 %collective-permute-done.3.t1_ref = f32[128,128]{1,0:T(8,128)S(1)} collective-permute-done((f32[128,128]{1,0:T(8,128)S(1)}, f32[128,128]{1,0:T(8,128)S(1)}, u32[]{:S(2)}, u32[]{:S(2)}) %collective-permute-start.3) | collective-permute-done | bytes 65568 | tf_op jit(solution)/shard_map/ppermute | solution.py:357
  84.6 1.4 %collective-permute-done.4.t2_ref = f32[128,128]{1,0:T(8,128)S(1)} collective-permute-done((f32[128,128]{1,0:T(8,128)S(1)}, f32[128,128]{1,0:T(8,128)S(1)}, u32[]{:S(2)}, u32[]{:S(2)}) %collective-permute-start.4) | collective-permute-done | bytes 65568 | tf_op jit(solution)/shard_map/ppermute | solution.py:357
  86.1 2.9 %recover.1 = f32[3,4,10368]{2,1,0:T(4,128)} custom-call(s32[2]{0:T(128)} %pad_add_fusion.at_ref, f32[128,128]{1,0:T(8,128)S(1)} %get-tuple-element.26.t0_ref, f32[128,128]{1,0:T(8,128)S(1)} %collective-permute-done.3.t1_ref, f32[128,128]{1,0:T(8,128)S(1)} %collective-permute-done.4.t2_ref, f32[128,128]{1,0:T(8,128)S(1)} %collective-permute-done.5.t3_ref, ...), custom_call_target="tpu_custom_call" | custom-call | tf_op jit(solution)/shard_map/recover/pallas_call | solution.py:342
  (59 shorter events, 0.2 us)
Async XLA Ops:
  2.7 15.6 %copy-start.24 = (f32[2,36,36]{2,0,1:T(2,128)S(1)}, f32[2,36,36]{2,0,1:T(2,128)}, u32[]{:S(2)}) copy-start(f32[2,36,36]{2,0,1:T(2,128)} %param.28) | copy-start | bytes 31108
  2.7 15.6 %copy-start.25 = (f32[2,36,81]{2,0,1:T(2,128)S(1)}, f32[2,36,81]{2,0,1:T(2,128)}, u32[]{:S(2)}) copy-start(f32[2,36,81]{2,0,1:T(2,128)} %param.29) | copy-start | bytes 69988
  2.7 15.7 %copy-start.26 = (f32[2,81,36]{1,0,2:T(2,128)S(1)}, f32[2,81,36]{1,0,2:T(2,128)}, u32[]{:S(2)}) copy-start(f32[2,81,36]{1,0,2:T(2,128)} %param.30) | copy-start | bytes 69988
  2.7 16.4 %copy-start.12 = (f32[256,81]{1,0:T(8,128)S(1)}, f32[256,81]{1,0:T(8,128)}, u32[]{:S(2)}) copy-start(f32[256,81]{1,0:T(8,128)} %constant.36.clone.node_ref) | copy-start | bytes 248836
  2.7 16.4 %copy-start.13 = (f32[128,256]{1,0:T(8,128)S(1)}, f32[128,256]{1,0:T(8,128)}, u32[]{:S(2)}) copy-start(f32[128,256]{1,0:T(8,128)} %constant.37.clone.mrn_ref) | copy-start | bytes 393220
  2.7 16.4 %copy-start.15 = (f32[128,36]{1,0:T(8,128)S(1)}, f32[128,36]{1,0:T(8,128)}, u32[]{:S(2)}) copy-start(f32[128,36]{1,0:T(8,128)} %constant.35.clone.edge_ref) | copy-start | bytes 55300
  2.7 16.4 %copy-start.16 = (f32[128,128]{1,0:T(8,128)S(1)}, f32[128,128]{1,0:T(8,128)}, u32[]{:S(2)}) copy-start(f32[128,128]{1,0:T(8,128)} %constant.38.clone.mrr_ref) | copy-start | bytes 196612
  2.8 16.4 %copy-start.17 = (f32[128,128]{1,0:T(8,128)S(1)}, f32[128,128]{1,0:T(8,128)}, u32[]{:S(2)}) copy-start(f32[128,128]{1,0:T(8,128)} %constant.39.clone.perm_ref) | copy-start | bytes 196612
  2.8 31.4 %copy-start.10 = (bf16[256,256]{1,0:T(8,128)(2,1)S(1)}, bf16[256,256]{1,0:T(8,128)(2,1)}, u32[]{:S(2)}) copy-start(bf16[256,256]{1,0:T(8,128)(2,1)} %constant.44.clone.ah_ref) | copy-start | bytes 393220
  2.8 31.4 %copy-start.11 = (bf16[256,256]{1,0:T(8,128)(2,1)S(1)}, bf16[256,256]{1,0:T(8,128)(2,1)}, u32[]{:S(2)}) copy-start(bf16[256,256]{1,0:T(8,128)(2,1)} %constant.45.clone.al_ref) | copy-start | bytes 393220
  2.8 31.4 %all-to-all-start = ((f32[64,16,128]{2,1,0:T(8,128)}), f32[64,16,128]{2,1,0:T(8,128)S(1)}, u32[]{:S(2)}, u32[]{:S(2)}) async-start(f32[64,16,128]{2,1,0:T(8,128)} %bitcast.2), calls=%async_computation | async-start | bytes 1048576 | tf_op jit(solution)/shard_map/all_to_all | solution.py:353
  18.3 15.8 %copy-start.4 = (bf16[256,512]{1,0:T(8,128)(2,1)S(1)}, bf16[256,512]{1,0:T(8,128)(2,1)}, u32[]{:S(2)}) copy-start(bf16[256,512]{1,0:T(8,128)(2,1)} %constant.43.clone.dl_ref) | copy-start | bytes 786436
  21.6 15.3 %copy-start.5 = (f32[256,256]{1,0:T(8,128)}, f32[256,256]{1,0:T(8,128)S(1)}, u32[]{:S(2)}) copy-start(f32[256,256]{1,0:T(8,128)S(1)} %get-tuple-element.19.lift_ref) | copy-start | bytes 786436
  21.6 36.3 %copy-start.18 = (f32[24,128]{1,0:T(8,128)}, f32[24,128]{1,0:T(8,128)S(1)}, u32[]{:S(2)}) copy-start(f32[24,128]{1,0:T(8,128)S(1)} %get-tuple-element.20.aux_ref) | copy-start | bytes 36868
  36.9 21.0 %copy-start.6 = (f32[256,256]{1,0:T(8,128)S(1)}, f32[256,256]{1,0:T(8,128)}, u32[]{:S(2)}) copy-start(f32[256,256]{1,0:T(8,128)} %copy-done.5) | copy-start | bytes 786436
  36.9 21.0 %copy-start.14 = (f32[128,24]{1,0:T(8,128)S(1)}, f32[128,24]{1,0:T(8,128)}, u32[]{:S(2)}) copy-start(f32[128,24]{1,0:T(8,128)} %constant.46.clone.place_ref) | copy-start | bytes 36868
  57.9 15.9 %copy-start.20 = (f32[64,128]{1,0:T(8,128)S(1)}, f32[64,128]{1,0:T(8,128)}, u32[]{:S(2)}) copy-start(f32[64,128]{1,0:T(8,128)} %constant.47.clone.pick_ref) | copy-start | bytes 98308
  59.3 26.8 %copy-start.8 = (f32[256,256]{1,0:T(8,128)S(1)}, f32[256,256]{1,0:T(8,128)}, u32[]{:S(2)}) copy-start(f32[256,256]{1,0:T(8,128)} %copy-done.7) | copy-start | bytes 786436
  59.3 11.2 %collective-permute-start = (f32[128,128]{1,0:T(8,128)S(1)}, f32[128,128]{1,0:T(8,128)S(1)}, u32[]{:S(2)}, u32[]{:S(2)}) collective-permute-start(f32[128,128]{1,0:T(8,128)S(1)} %get-tuple-element.22), channel_id=1, source_target_pairs={{0,1},{1,2},{2,3},{3,0},{4,5},{5,6},{6,7},{7,4},{8,9},{9,10},{10,1... | collective-permute-start | bytes 196616 | tf_op jit(solution)/shard_map/ppermute | solution.py:357
  67.2 6.6 %collective-permute-start.1 = (f32[128,128]{1,0:T(8,128)S(1)}, f32[128,128]{1,0:T(8,128)S(1)}, u32[]{:S(2)}, u32[]{:S(2)}) collective-permute-start(f32[128,128]{1,0:T(8,128)S(1)} %get-tuple-element.23), channel_id=1, source_target_pairs={{0,2},{1,3},{2,0},{3,1},{4,6},{5,7},{6,4},{7,5},{8,10},{9,11},{10,... | collective-permute-start | bytes 196616 | tf_op jit(solution)/shard_map/ppermute | solution.py:357
  67.7 6.1 %collective-permute-start.2 = (f32[128,128]{1,0:T(8,128)S(1)}, f32[128,128]{1,0:T(8,128)S(1)}, u32[]{:S(2)}, u32[]{:S(2)}) collective-permute-start(f32[128,128]{1,0:T(8,128)S(1)} %get-tuple-element.24), channel_id=1, source_target_pairs={{0,3},{1,0},{2,1},{3,2},{4,7},{5,4},{6,5},{7,6},{8,11},{9,8},{10,9... | collective-permute-start | bytes 196616 | tf_op jit(solution)/shard_map/ppermute | solution.py:357
  77.8 6.8 %collective-permute-start.3 = (f32[128,128]{1,0:T(8,128)S(1)}, f32[128,128]{1,0:T(8,128)S(1)}, u32[]{:S(2)}, u32[]{:S(2)}) collective-permute-start(f32[128,128]{1,0:T(8,128)S(1)} %get-tuple-element.27), channel_id=1, source_target_pairs={{0,1},{1,2},{2,3},{3,0},{4,5},{5,6},{6,7},{7,4},{8,9},{9,10},{10,1... | collective-permute-start | bytes 196616 | tf_op jit(solution)/shard_map/ppermute | solution.py:357
  79.3 6.8 %collective-permute-start.4 = (f32[128,128]{1,0:T(8,128)S(1)}, f32[128,128]{1,0:T(8,128)S(1)}, u32[]{:S(2)}, u32[]{:S(2)}) collective-permute-start(f32[128,128]{1,0:T(8,128)S(1)} %get-tuple-element.28), channel_id=1, source_target_pairs={{0,2},{1,3},{2,0},{3,1},{4,6},{5,7},{6,4},{7,5},{8,10},{9,11},{10,... | collective-permute-start | bytes 196616 | tf_op jit(solution)/shard_map/ppermute | solution.py:357
  81.3 4.7 %collective-permute-start.5 = (f32[128,128]{1,0:T(8,128)S(1)}, f32[128,128]{1,0:T(8,128)S(1)}, u32[]{:S(2)}, u32[]{:S(2)}) collective-permute-start(f32[128,128]{1,0:T(8,128)S(1)} %get-tuple-element.29), channel_id=1, source_target_pairs={{0,3},{1,0},{2,1},{3,2},{4,7},{5,4},{6,5},{7,6},{8,11},{9,8},{10,9... | collective-permute-start | bytes 196616 | tf_op jit(solution)/shard_map/ppermute | solution.py:357
  (11 other events, 91.9 us)

commit v2 on v0

v2 whole, which is shorter than its diff:
```python
import functools

import jax
import jax.numpy as jnp
import ml_dtypes
import numpy as np
from jax import lax
from jax.experimental import pallas as pl
from jax.experimental.pallas import tpu as pltpu
from jax.sharding import PartitionSpec as P

PLANES = 256
QUAD = 9
NODE = QUAD * QUAD
GROUPS = 64
PARTS = 4
PART_NODES = 10368
CG_STEPS = 4
BETA_COEF = 0.01
STEP_DT = 0.002
HIGHEST = lax.Precision.HIGHEST
F32 = jnp.float32
BF16 = jnp.bfloat16


def gauss_derivative(points):
    nodes = -np.cos(np.pi * (2 * np.arange(points) + 1) / (2 * points))
    ident = np.eye(points)
    diffs = nodes[:, None] - nodes[None, :] + ident
    weights = 1.0 / np.prod(diffs, axis=1)
    matrix = (weights[None, :] / weights[:, None]) / diffs
    matrix = matrix * (1.0 - ident)
    return matrix - ident * matrix.sum(axis=1)[:, None]


def split_np(table):
    high = table.astype(np.float32).astype(ml_dtypes.bfloat16)
    low = (table - high.astype(np.float64)).astype(np.float32).astype(ml_dtypes.bfloat16)
    return high, low


@functools.lru_cache(None)
def tables():
    z = np.arange(PLANES)
    rows = np.arange(PLANES)
    waves = (rows + 1) // 2
    angle = 2.0 * np.pi / PLANES * (waves[None, :] * z[:, None] % PLANES)
    cosine, sine = np.cos(angle), np.sin(angle)
    odd = (rows % 2 == 1)[None, :]
    ends = ((rows == 0) | (rows == PLANES - 1))[None, :]
    synth = np.where((rows == 0)[None, :], 1.0, np.where(odd, cosine, sine))
    rate = BETA_COEF * waves[None, :]
    slope = np.where(ends, 0.0, np.where(odd, -rate * sine, rate * cosine))
    weight = np.where(ends[0], 1.0 / PLANES, 2.0 / PLANES)
    analysis = synth.T * weight[:, None]
    deriv = gauss_derivative(QUAD)
    first = np.kron(deriv, np.eye(QUAD))
    second = np.kron(np.eye(QUAD), deriv)
    both = np.zeros((256, 512))
    for c in range(3):
        at = slice(c * NODE, (c + 1) * NODE)
        both[at, c * NODE:(c + 1) * NODE] = first.T
        both[at, 256 + c * NODE:256 + (c + 1) * NODE] = second.T
    out = []
    for table in (np.concatenate([synth, slope], 0), both, analysis):
        out.extend(split_np(table))
    return tuple(out)


@functools.lru_cache(None)
def selections():
    edge = np.zeros((128, 36), np.float32)
    node = np.zeros((256, NODE), np.float32)
    comp_row = np.full(128, -1)
    comp_col = np.full(256, -2)
    for c in range(3):
        for s in range(4):
            for k in range(QUAD):
                edge[s * 32 + c * QUAD + k, s * QUAD + k] = 1
                comp_row[s * 32 + c * QUAD + k] = c
        for n in range(NODE):
            node[c * NODE + n, n] = 1
            comp_col[c * NODE + n] = c
    mask_rn = (comp_row[:, None] == comp_col[None, :]).astype(np.float32)
    mask_rr = ((comp_row[:, None] == comp_row[None, :]) & (comp_row >= 0)[:, None]).astype(np.float32)
    perm = np.zeros((128, 128), np.float32)
    for p in range(GROUPS):
        for el in range(2):
            perm[2 * p + el, el * GROUPS + p] = 1
    pick = np.zeros((64, 24), np.float32)
    for c in range(3):
        for k in range(QUAD):
            pick[c * QUAD + k, 2 + k] = 1
            pick[32 + c * QUAD + k, 11 + k] = 1
    return edge, node, mask_rn, mask_rr, perm, pick


def split(x):
    high = x.astype(BF16)
    return high, (x - high.astype(F32)).astype(BF16)


def dot3(a, b, dims=(((1,), (0,)), ((), ()))):
    mul = functools.partial(lax.dot_general, dimension_numbers=dims, preferred_element_type=F32)
    return mul(a[0], b[0]) + (mul(a[0], b[1]) + mul(a[1], b[0]))


def dot6(a, b, dims=(((1,), (0,)), ((), ()))):
    return lax.dot_general(a, b, dims, precision=HIGHEST, preferred_element_type=F32)


NT = (((1,), (1,)), ((), ()))


PACK_STEPS = 2
PACK_ELEMS = 2 * GROUPS // PACK_STEPS


def window_base(e):
    return min(NODE * e // 128 * 128, PART_NODES - 256)


PACK_CUTS = (0,) + tuple(window_base(PACK_ELEMS * (g + 1) - 1) + 256 for g in range(PACK_STEPS))


def pack_kernel(v_ref, o_ref, v_scr, o_scr, in_sems, out_sems):
    lane = lax.broadcasted_iota(jnp.int32, (4, 256), 1)

    def arriving(g):
        cols = slice(PACK_CUTS[g], PACK_CUTS[g + 1])
        return pltpu.make_async_copy(v_ref.at[:, :, cols], v_scr.at[:, :, cols], in_sems.at[g])

    def leaving(g):
        rows = slice(8 * PACK_ELEMS * g, 8 * PACK_ELEMS * (g + 1))
        return pltpu.make_async_copy(o_scr.at[rows], o_ref.at[rows], out_sems.at[g])

    for g in range(PACK_STEPS):
        arriving(g).start()
    for g in range(PACK_STEPS):
        arriving(g).wait()
        for e in range(PACK_ELEMS * g, PACK_ELEMS * (g + 1)):
            start = NODE * e
            base = window_base(e)
            rows = jnp.zeros((4, 256), F32)
            for c in range(3):
                window = v_scr[c, :, base:base + 256]
                turned = pltpu.roll(window, (NODE * c - (start - base)) % 256, 1)
                rows = jnp.where((lane >= NODE * c) & (lane < NODE * (c + 1)), turned, rows)
            at = 16 * (e // 2) + 4 * (e % 2)
            o_scr[at:at + 4, :] = rows[:, :128]
            o_scr[at + 8:at + 12, :] = rows[:, 128:]
        leaving(g).start()
    for g in range(PACK_STEPS):
        leaving(g).wait()


def prep_kernel(geo_ref, kind_ref, scale_ref, dir_ref, stiff_ref, mass_ref, lift_ref, rec_ref,
                edge_ref, node_ref, mrn_ref, mrr_ref, perm_ref,
                lift_out, w_out, rec_out, geo_out, aux_out, aux_scr):
    place = lax.axis_index("planes")
    lane = lax.broadcasted_iota(jnp.int32, (4, 256), 1)
    for el in range(2):
        start = 2 * NODE * place + NODE * el
        base = pl.multiple_of(jnp.minimum(lax.div(start, 128) * 128, PART_NODES - 256), 128)
        window = geo_ref[:, pl.ds(base, 256)]
        turned = pltpu.roll(window, lax.rem(256 - (start - base), 256), 1)
        tiled = jnp.where(lane < NODE, turned,
                          jnp.where(lane < 2 * NODE, pltpu.roll(turned, NODE, 1), pltpu.roll(turned, 2 * NODE, 1)))
        geo_out[4 * el:4 * el + 4, :] = jnp.where(lane < 3 * NODE, tiled, 0.0)
    wave = lax.div(4 * place + lax.axis_index("elem") + 1, 2).astype(F32)
    lam = 1.0 + (BETA_COEF * wave) * (BETA_COEF * wave)
    edge = edge_ref[...]
    node = node_ref[...]
    for t in range(2):
        rows = slice(128 * t, 128 * (t + 1))
        lift_out[rows, :] = dot6(dot6(edge, lift_ref[t]), node, NT) * mrn_ref[...]
        rec_out[rows, :] = dot6(dot6(edge, rec_ref[t], NT), node, NT) * mrn_ref[...]
        mixed = stiff_ref[t] + lam * mass_ref[t]
        w_out[:, rows] = dot6(dot6(edge, mixed), edge, NT) * mrr_ref[...]
    second = (kind_ref[...] == 1).astype(F32)
    aux_scr[...] = jnp.zeros((24, 128), F32)
    aux_scr[0:1, :] = scale_ref[...] * (1.0 - second)
    aux_scr[1:2, :] = scale_ref[...] * second
    aux_scr[2:11, :] = (1 - dir_ref[0]).astype(F32)
    aux_scr[11:20, :] = (1 - dir_ref[1]).astype(F32)
    aux_scr[20:21, :] = second
    aux_out[...] = dot6(aux_scr[...], perm_ref[...])


def swap_halves(x, y):
    first = lax.broadcasted_iota(jnp.int32, x.shape, 1) < 4
    return jnp.where(first, x, pltpu.roll(y, 4, 1)), jnp.where(first, pltpu.roll(x, 4, 1), y)


def advect_kernel(x_ref, th_ref, tl_ref, dh_ref, dl_ref, ah_ref, al_ref, geo_ref, o_ref, items_scr, synth_scr, adv_scr):
    lane = lax.broadcasted_iota(jnp.int32, (256, 256), 1)
    low = lane < NODE
    mid = lane < 2 * NODE
    for t in range(2):
        pairs = [jnp.concatenate([x_ref[32 * m + 16 * odd + 8 * t:32 * m + 16 * odd + 8 * t + 8, :] for m in range(32)], axis=0)
                 .reshape(32, 8, 128) for odd in range(2)]
        for el, rows in enumerate(swap_halves(*pairs)):
            items_scr[256 * el:256 * (el + 1), 128 * t:128 * (t + 1)] = rows.reshape(256, 128)
    for el in range(2):
        here = slice(256 * el, 256 * (el + 1))
        synth_scr[...] = dot3((th_ref[...], tl_ref[...]), split(items_scr[here, :]))
        geo = geo_ref[4 * el:4 * el + 4, :]
        values = synth_scr[:256, :]
        both = dot3(split(values), (dh_ref[...], dl_ref[...]))
        along_r = both[:, :256]
        along_s = both[:, 256:]
        along_x = geo[0:1] * along_r + geo[1:2] * along_s
        along_y = geo[2:3] * along_r + geo[3:4] * along_s
        up = pltpu.roll(values, NODE, 1)
        up2 = pltpu.roll(values, 2 * NODE, 1)
        down = pltpu.roll(values, 256 - NODE, 1)
        down2 = pltpu.roll(values, 256 - 2 * NODE, 1)
        u = jnp.where(low, values, jnp.where(mid, up, up2))
        v = jnp.where(low, down, jnp.where(mid, values, up))
        w = jnp.where(low, down2, jnp.where(mid, down, values))
        adv_scr[...] = u * along_x + v * along_y + w * synth_scr[256:, :]
        hat = dot3((ah_ref[...], al_ref[...]), split(adv_scr[...]))
        items_scr[here, :] = items_scr[here, :] - STEP_DT * hat
    for t in range(2):
        elems = [items_scr[256 * el:256 * (el + 1), 128 * t:128 * (t + 1)].reshape(32, 8, 128) for el in range(2)]
        for odd, rows in enumerate(swap_halves(*elems)):
            for m in range(32):
                at = 32 * m + 16 * odd + 8 * t
                o_ref[at:at + 8, :] = rows[m]


def turn(x, shift):
    return pltpu.roll(x, shift % 128, 1)


def lanes(rows):
    lane = lax.broadcasted_iota(jnp.int32, (rows, 128), 1)
    p = lane & 63
    el = lane >> 6
    return p, el, 2 * (p & 15) + el


def fold(x, first):
    group = lanes(8)[0] >> 4
    out = jnp.zeros((8, 128), F32)
    for g in range(4):
        out = jnp.where(group == g, turn(x[8 * g:8 * g + 8], 16 * g - first), out)
    return out


def unfold(x, first):
    return jnp.concatenate([turn(x, first - 16 * g) for g in range(4)], axis=0)


def take_top(h):
    p, el, height = lanes(32)
    return jnp.where(height == 31, 0.0, jnp.where(el == 0, turn(h, 64), turn(h, 63)))


def give_top(h):
    p, el, height = lanes(32)
    return jnp.where(height == 0, 0.0, jnp.where(el == 1, turn(h, 64), turn(h, -63)))


def lift_kernel(x_ref, lift_ref, aux_ref, o0_ref, o1_ref, o2_ref, o3_ref, in_scr, out_scr):
    arrived = jnp.transpose(x_ref[...].reshape(GROUPS, 16, 128), (1, 0, 2))
    for q in range(4):
        for el in range(2):
            at = (2 * q + el) * 64
            for t in range(2):
                in_scr[at:at + 64, t * 128:(t + 1) * 128] = arrived[t * 8 + el * 4 + q]
    lifted = dot3(split(lift_ref[...]), split(in_scr[...]), NT)
    second = aux_ref[20:21, :] > 0.5
    p = lanes(32)[0]
    for q in range(4):
        cols = slice(128 * q, 128 * (q + 1))
        edges = jnp.where(second, lifted[128:, cols], lifted[:128, cols])
        right = edges[32:64]
        out_scr[q, 0:32] = edges[0:32] + jnp.where(p >= 16, turn(right, 16), 0.0)
        out_scr[q, 32:64] = edges[64:96] + give_top(edges[96:128])
        out_scr[q, 64:72] = fold(right, 48)
        out_scr[q, 72:96] = aux_ref[...]
    for k, ref in enumerate((o0_ref, o1_ref, o2_ref, o3_ref)):
        ref[...] = out_scr[lax.rem(lax.axis_index("elem") + k, PARTS)]


def cg_kernel(f0_ref, f1_ref, f2_ref, f3_ref, w_ref, pick_ref, o0_ref, o1_ref, o2_ref, o3_ref, scr):
    for k, ref in enumerate((f0_ref, f1_ref, f2_ref, f3_ref)):
        scr[lax.rem(lax.axis_index("elem") + PARTS - k, PARTS)] = ref[...]
    p = lanes(32)[0]
    sub = lax.broadcasted_iota(jnp.int32, (64, 1), 0) & 31
    comp = (sub >= QUAD).astype(jnp.int32) + (sub >= 2 * QUAD).astype(jnp.int32)
    zero = jnp.zeros((32, 128), F32)

    def parts(x):
        return [x[:, 128 * i:128 * (i + 1)] for i in range(PARTS)]

    def right_of(v):
        v = parts(v)
        return jnp.concatenate([jnp.where(p < 48, turn(v[i], -16), turn(v[i + 1], 48) if i < 3 else zero)
                                for i in range(PARTS)], axis=1)

    def from_left(v):
        v = parts(v)
        return jnp.concatenate([jnp.where(p >= 16, turn(v[i], 16), turn(v[i - 1], -48) if i > 0 else zero)
                                for i in range(PARTS)], axis=1)

    def top_of(h):
        return jnp.concatenate([take_top(x) for x in parts(h)], axis=1)

    def from_below(h):
        return jnp.concatenate([give_top(x) for x in parts(h)], axis=1)

    def vector_of(x):
        v, h = x[:32], x[32:]
        return jnp.concatenate([v, right_of(v), h, top_of(h)], axis=0)

    aux = jnp.concatenate([scr[i, 72:96] for i in range(PARTS)], axis=1)
    free = dot6(pick_ref[...], aux)
    first_scale = aux[0:1]
    second_scale = aux[1:2]
    w_high, w_low = split(w_ref[...])
    w_both = jnp.concatenate([w_high, w_low], axis=0)

    def operator(x):
        high, low = split(x)
        both = lax.dot(w_both, high, preferred_element_type=F32)
        return both[:128] + (both[128:] + lax.dot(w_high, low, preferred_element_type=F32))

    def assemble(y):
        return jnp.concatenate([y[:32] + from_left(y[32:64]), y[64:96] + from_below(y[96:])], axis=0) * free

    def total(a, b):
        line = jnp.sum(a * b, axis=1, keepdims=True)
        sums = [jnp.sum(jnp.where(comp == c, line, 0.0), axis=0, keepdims=True) for c in range(3)]
        return jnp.where(comp == 0, sums[0], jnp.where(comp == 1, sums[1], sums[2]))

    sent = []
    for i in range(PARTS):
        v = scr[i, 0:32]
        if i > 0:
            v = v + jnp.where(p < 16, unfold(scr[i - 1, 64:72], 0), 0.0)
        sent.append(jnp.concatenate([v, scr[i, 32:64]], axis=0))
    residual = jnp.concatenate(sent, axis=1) * free
    direction = residual
    trace = jnp.zeros_like(residual)
    now = total(residual, residual)
    for step in range(CG_STEPS):
        vector = vector_of(direction)
        image = assemble(operator(jnp.concatenate([vector * first_scale, vector * second_scale], axis=0)))
        alpha = now / total(direction, image)
        trace = trace + alpha * direction
        if step + 1 < CG_STEPS:
            residual = residual - alpha * image
            fresh = total(residual, residual)
            direction = residual + (fresh / now) * direction
            now = fresh
    pieces = parts(trace)
    for i in range(PARTS):
        scr[i, 0:64] = pieces[i]
        scr[i, 64:72] = fold(pieces[i + 1][:32], 0) if i < 3 else jnp.zeros((8, 128), F32)
    for k, ref in enumerate((o0_ref, o1_ref, o2_ref, o3_ref)):
        ref[...] = scr[lax.rem(lax.axis_index("elem") + k, PARTS), 0:72]


def recover_kernel(t0_ref, t1_ref, t2_ref, t3_ref, x_ref, rec_ref, aux_ref, o_ref, scr, t_scr, o_scr, sems):
    for k, ref in enumerate((t0_ref, t1_ref, t2_ref, t3_ref)):
        t_scr[lax.rem(lax.axis_index("elem") + PARTS - k, PARTS), 0:72] = ref[...]
    second = aux_ref[20:21, :]
    p = lanes(32)[0]
    row = lax.broadcasted_iota(jnp.int32, (32, 128), 0)
    vectors = []
    for q in range(4):
        v = t_scr[q, 0:32]
        h = t_scr[q, 32:64]
        right = jnp.where(p < 48, turn(v, -16), unfold(t_scr[q, 64:72], 48))
        vectors.append(jnp.concatenate([v, right, h, jnp.where(row == 31, second, take_top(h))], axis=0))
    turned = jnp.concatenate(vectors, axis=1).T
    kind = turned[:, 127:128]
    recovered = dot3(split(jnp.concatenate([turned * (1.0 - kind), turned * kind], axis=1)), split(rec_ref[...]))
    wave = lax.div(4 * lax.axis_index("planes") + (lax.broadcasted_iota(jnp.int32, (8, 128), 0) & 3) + 1, 2).astype(F32)
    weight = 1.0 / (2.0 + (BETA_COEF * wave) * (BETA_COEF * wave))
    for t in range(2):
        pieces = [recovered[(2 * q + el) * 64:(2 * q + el + 1) * 64, 128 * t:128 * (t + 1)] for el in range(2) for q in range(4)]
        mine = jnp.transpose(jnp.concatenate(pieces, axis=0).reshape(8, GROUPS, 128), (1, 0, 2))
        for g in range(GROUPS):
            scr[512 * t + 8 * g:512 * t + 8 * g + 8, :] = x_ref[16 * g + 8 * t:16 * g + 8 * t + 8, :] * weight + mine[g]
    lane = lax.broadcasted_iota(jnp.int32, (4, 128), 1)

    def leaving(c):
        return pltpu.make_async_copy(o_scr.at[c], o_ref.at[c], sems.at[c])

    for c in range(3):
        current = jnp.zeros((4, 128), F32)
        for e in range(2 * GROUPS):
            tile, offset = divmod(NODE * e, 128)
            rows = jnp.concatenate([scr[4 * e:4 * e + 4, :], scr[512 + 4 * e:516 + 4 * e, :]], axis=1)
            turned = pltpu.roll(rows, (offset - NODE * c) % 256, 1)
            current = jnp.where(lane >= offset, turned[:, :128], current)
            if offset + NODE >= 128:
                o_scr[c, :, 128 * tile:128 * (tile + 1)] = current
                current = turned[:, 128:]
        leaving(c).start()
    for c in range(3):
        leaving(c).wait()


VMEM = pl.BlockSpec(memory_space=pltpu.VMEM)


def shape(*dims):
    return jax.ShapeDtypeStruct(dims, F32)


ANY = pl.BlockSpec(memory_space=pl.ANY)


def call(kernel, name, out, args, scratch=(), sems=(), far_in=False, far_out=False):
    many = isinstance(out, tuple)
    if not far_in:
        args = tuple(pltpu.with_memory_space_constraint(jnp.asarray(a), pltpu.VMEM) for a in args)
    if not far_out:
        outs = tuple(pltpu.VMEM(o.shape, F32) for o in (out if many else (out,)))
        out = outs if many else outs[0]
    place = ANY if far_out else VMEM
    return pl.pallas_call(
        kernel,
        name=name,
        out_shape=out,
        in_specs=[ANY if far_in else VMEM] * len(args),
        out_specs=tuple(place for _ in out) if many else place,
        scratch_shapes=[pltpu.VMEM(dims, F32) for dims in scratch] + [pltpu.SemaphoreType.DMA((n,)) for n in sems],
    )(*args)


def exchange(value, axis, count):
    return lax.all_to_all(value.reshape(count, -1, 128), axis, split_axis=0, concat_axis=0, tiled=True)


def spread(blocks):
    moved = [lax.ppermute(blocks[k], "elem", [(s, (s + k) % PARTS) for s in range(PARTS)]) for k in range(1, PARTS)]
    return (blocks[0],) + tuple(moved)


def per_device(velocity, geometry, element_kind, element_scale, dirichlet, schur_stiffness, schur_mass, lift, recover):
    edge, node, mask_rn, mask_rr, perm, pick = selections()
    packed = call(pack_kernel, "pack", shape(1024, 128), (velocity,),
                  scratch=((3, 4, PART_NODES), (1024, 128)), sems=(PACK_STEPS, PACK_STEPS), far_in=True, far_out=True)
    arrived = exchange(packed, "planes", GROUPS).reshape(1024, 128)
    lift_all, w_all, rec_all, geo, aux = call(
        prep_kernel, "prep",
        (shape(256, 256), shape(128, 256), shape(256, 256), shape(8, 256), shape(24, 128)),
        (geometry, element_kind.reshape(1, 128), element_scale.reshape(1, 128), dirichlet,
         schur_stiffness, schur_mass, lift, recover, edge, node, mask_rn, mask_rr, perm),
        scratch=((24, 128),))
    inter = call(advect_kernel, "advect", shape(1024, 128), (arrived,) + tables() + (geo,),
                 scratch=((512, 256), (512, 256), (256, 256)))
    owned = exchange(inter, "planes", GROUPS).reshape(1024, 128)
    lifted = call(lift_kernel, "lift", (shape(96, 128),) * PARTS, (owned, lift_all, aux),
                  scratch=((512, 256), (PARTS, 96, 128)))
    traces = call(cg_kernel, "cg", (shape(72, 128),) * PARTS, spread(lifted) + (w_all, pick),
                  scratch=((PARTS, 96, 128),))
    return call(recover_kernel, "recover", shape(3, 4, PART_NODES), spread(traces) + (owned, rec_all, aux),
                scratch=((1024, 128), (PARTS, 96, 128), (3, 4, PART_NODES)), sems=(3,), far_out=True)


def solution(mesh):
    in_specs = (
        P(None, "planes", "elem"),
        P(None, "elem"),
        P("elem"),
        P("elem"),
        P(None, None, "elem"),
        P(),
        P(),
        P(),
        P(),
    )
    out_specs = P(None, "planes", "elem")
    return jax.shard_map(per_device, mesh=mesh, in_specs=in_specs, out_specs=out_specs, check_vma=False)
```

time: 105 us -> 85.6 us (0.82)
  blocking collectives: 53.5 us -> 21 us
  starting transfers between devices: 14.7 us -> 30.1 us
  waiting for transfers between devices: 8.65 us -> 20.4 us
  Pallas kernels: 21.6 us -> 12.4 us
  local copies, waits for them, and re-layouts: 4.6 us -> 0.93 us
    all_to_all x3 -> x1, blocking collectives: 53.5 us -> 21 us  [exchange(): lax.all_to_all(value.reshape(count, -1, 128), axis, split_axis=0, concat_...]
    ppermute x0 -> x6, starting transfers between devices: none -> 15.4 us  [spread(): lax.ppermute(blocks[k], 'elem', [(s, (s + k) % PARTS) for s in range(PART...]
    pallas_call x6, Pallas kernels: 21.6 us -> 12.4 us  [call(): pl.pallas_call(kernel, name=name, out_shape=out, in_specs=[ANY if far_in...]
    ppermute x0 -> x6, waiting for transfers between devices: none -> 6.29 us  [spread(): lax.ppermute(blocks[k], 'elem', [(s, (s + k) % PARTS) for s in range(PART...]
    all_to_all x1, waiting for transfers between devices: 8.65 us -> 14.1 us  [exchange(): lax.all_to_all(value.reshape(count, -1, 128), axis, split_axis=0, concat_...]
    unnamed x17 -> x53, local copies, waits for them, and re-layouts: 4.6 us -> 0.93 us
  transfers between devices with their start and end apart: 1 -> 7, of which waited for: 1 -> 5; matrix products, arithmetic and copies ran while one was open for 4% -> 0% of each run, Pallas kernels for 3% -> 2%
where the time goes in v2:
time: 85.6 us; the launch traced here: 85.2 us
  starting transfers between devices  30.1 us (35%)
  blocking collectives  21 us (25%)
  waiting for transfers between devices  20.4 us (24%)
  Pallas kernels  12.4 us (14%)
  local copies, waits for them, and re-layouts  0.93 us (1%)
    all_to_all x1, blocking collectives, exchange(): lax.all_to_all(value.reshape(count, -1, 128), axis, split_axis=0, concat_...  21 us
    ppermute x6, starting transfers between devices, spread(): lax.ppermute(blocks[k], 'elem', [(s, (s + k) % PARTS) for s in range(PART...  15.4 us
    all_to_all x1, starting transfers between devices, exchange(): lax.all_to_all(value.reshape(count, -1, 128), axis, split_axis=0, concat_...  14.7 us
    all_to_all x1, waiting for transfers between devices, exchange(): lax.all_to_all(value.reshape(count, -1, 128), axis, split_axis=0, concat_...  14.1 us
    pallas_call x6, Pallas kernels, call(): pl.pallas_call(kernel, name=name, out_shape=out, in_specs=[ANY if far_in...  12.4 us
    ppermute x6, waiting for transfers between devices, spread(): lax.ppermute(blocks[k], 'elem', [(s, (s + k) % PARTS) for s in range(PART...  6.29 us
  transfers between devices with their start and end apart: 7, of which 5 were waited for; matrix products, arithmetic and copies ran while one was open for 0% of the time, Pallas kernels for 2%

profile of v2, /device:TPU:8, one launch (start us, length us, event | category | flops | bytes accessed | tf_op | source)
XLA Modules:
  0.0 85.2 jit_solution(13706740652276190845)
XLA Ops:
  0.0 2.6 %pack.1 = f32[1024,128]{1,0:T(8,128)} custom-call(f32[3,4,10368]{2,1,0:T(4,128)} %v_ref.1), custom_call_target="tpu_custom_call" | custom-call | tf_op jit(solution)/shard_map/pack/pallas_call | solution.py:426
  2.7 0.0 copy-start.11
  2.7 0.0 copy-start.13
  2.7 0.0 copy-start.14
  2.8 14.7 %all-to-all-start = ((f32[64,16,128]{2,1,0:T(8,128)}), f32[64,16,128]{2,1,0:T(8,128)S(1)}, u32[]{:S(2)}, u32[]{:S(2)}) async-start(f32[64,16,128]{2,1,0:T(8,128)} %bitcast.12), calls=%async_computation | async-start | bytes 1048576 | tf_op jit(solution)/shard_map/all_to_all | solution.py:437
  17.6 0.1 copy.26.rec_ref
  17.8 0.6 copy-done.8
  18.5 1.5 %prep.1 = (f32[256,256]{1,0:T(8,128)S(1)}, f32[128,256]{1,0:T(8,128)S(1)}, f32[256,256]{1,0:T(8,128)S(1)}, f32[8,256]{1,0:T(8,128)S(1)}, f32[24,128]{1,0:T(8,128)S(1)}) custom-call(f32[4,10368]{1,0:T(4,128)S(1)} %copy-done.8, s32[1,128]{1,0:T(1,128)S(1)} %bitcast.10, f32[1,128]{1,0:T(1,128)S(1)} %bitcast.11, s32[2,9,128]{2,1,0:T(8,128)S(1)} %copy.22.dir_ref, ...), custom_call_target="tpu_custom_call" | custom-call | tf_op jit(solution)/shard_map/prep/pallas_call | solution.py:426
  20.0 14.1 %all-to-all-done = f32[64,16,128]{2,1,0:T(8,128)S(1)} async-done(((f32[64,16,128]{2,1,0:T(8,128)}), f32[64,16,128]{2,1,0:T(8,128)S(1)}, u32[]{:S(2)}, u32[]{:S(2)}) %all-to-all-start) | async-done | bytes 524320 | tf_op jit(solution)/shard_map/all_to_all | solution.py:437
  34.2 2.2 %advect.1 = f32[1024,128]{1,0:T(8,128)S(1)} custom-call(f32[1024,128]{1,0:T(8,128)S(1)} %bitcast.8, bf16[512,256]{1,0:T(8,128)(2,1)S(1)} %copy-done, bf16[512,256]{1,0:T(8,128)(2,1)S(1)} %copy-done.1, bf16[256,512]{1,0:T(8,128)(2,1)S(1)} %copy-done.2, bf16[256,512]{1,0:T(8,128)(2,1)S(1)} %copy-done.3, bf16[256,256]{1,0:T(8,128)(2,1)S(1)} %copy-done.9, ...), custom_call_target="tpu_custom_call" | custom-call | tf_op jit(solution)/shard_map/advect/pallas_call | solution.py:426
  36.5 21.0 %all_to_all.10 = f32[64,16,128]{2,1,0:T(8,128)S(1)} all-to-all(f32[64,16,128]{2,1,0:T(8,128)S(1)} %bitcast.9), channel_id=1, replica_groups=mesh['planes'=64,'elem'=4] {'planes'}, dimensions={0} | all-to-all | bytes 1048576 | tf_op jit(solution)/shard_map/all_to_all | solution.py:437
  57.5 0.6 lift.1
  58.1 8.0 %collective-permute-start = (f32[96,128]{1,0:T(8,128)S(1)}, f32[96,128]{1,0:T(8,128)S(1)}, u32[]{:S(2)}, u32[]{:S(2)}) collective-permute-start(f32[96,128]{1,0:T(8,128)S(1)} %get-tuple-element.22), channel_id=1, source_target_pairs={{0,1},{1,2},{2,3},{3,0},{4,5},{5,6},{6,7},{7,4},{8,9},{9,10},{10,1... | collective-permute-start | bytes 147464 | tf_op jit(solution)/shard_map/ppermute | solution.py:441
  66.1 0.4 collective-permute-start.1
  66.5 2.8 %collective-permute-start.2 = (f32[96,128]{1,0:T(8,128)S(1)}, f32[96,128]{1,0:T(8,128)S(1)}, u32[]{:S(2)}, u32[]{:S(2)}) collective-permute-start(f32[96,128]{1,0:T(8,128)S(1)} %get-tuple-element.24), channel_id=1, source_target_pairs={{0,3},{1,0},{2,1},{3,2},{4,7},{5,4},{6,5},{7,6},{8,11},{9,8},{10,9... | collective-permute-start | bytes 147464 | tf_op jit(solution)/shard_map/ppermute | solution.py:441
  69.3 2.6 %collective-permute-done.1.f2_ref = f32[96,128]{1,0:T(8,128)S(1)} collective-permute-done((f32[96,128]{1,0:T(8,128)S(1)}, f32[96,128]{1,0:T(8,128)S(1)}, u32[]{:S(2)}, u32[]{:S(2)}) %collective-permute-start.1) | collective-permute-done | bytes 49184 | tf_op jit(solution)/shard_map/ppermute | solution.py:441
  71.9 3.0 %cg.1 = (f32[72,128]{1,0:T(8,128)S(1)}, f32[72,128]{1,0:T(8,128)S(1)}, f32[72,128]{1,0:T(8,128)S(1)}, f32[72,128]{1,0:T(8,128)S(1)}) custom-call(f32[96,128]{1,0:T(8,128)S(1)} %get-tuple-element.21.f0_ref, f32[96,128]{1,0:T(8,128)S(1)} %collective-permute-done.f1_ref, f32[96,128]{1,0:T(8,128)S(1)} %collective-permute-done.1.f2_ref, ...), custom_call_target="tpu_custom_call" | custom-call | tf_op jit(solution)/shard_map/cg/pallas_call | solution.py:426
  74.9 1.2 %collective-permute-start.3 = (f32[72,128]{1,0:T(8,128)S(1)}, f32[72,128]{1,0:T(8,128)S(1)}, u32[]{:S(2)}, u32[]{:S(2)}) collective-permute-start(f32[72,128]{1,0:T(8,128)S(1)} %get-tuple-element.27), channel_id=1, source_target_pairs={{0,1},{1,2},{2,3},{3,0},{4,5},{5,6},{6,7},{7,4},{8,9},{9,10},{10,1... | collective-permute-start | bytes 110600 | tf_op jit(solution)/shard_map/ppermute | solution.py:441
  76.1 2.8 %collective-permute-start.4 = (f32[72,128]{1,0:T(8,128)S(1)}, f32[72,128]{1,0:T(8,128)S(1)}, u32[]{:S(2)}, u32[]{:S(2)}) collective-permute-start(f32[72,128]{1,0:T(8,128)S(1)} %get-tuple-element.28), channel_id=1, source_target_pairs={{0,2},{1,3},{2,0},{3,1},{4,6},{5,7},{6,4},{7,5},{8,10},{9,11},{10,... | collective-permute-start | bytes 110600 | tf_op jit(solution)/shard_map/ppermute | solution.py:441
  78.9 0.3 collective-permute-start.5
  79.1 1.7 %collective-permute-done.3.t1_ref = f32[72,128]{1,0:T(8,128)S(1)} collective-permute-done((f32[72,128]{1,0:T(8,128)S(1)}, f32[72,128]{1,0:T(8,128)S(1)}, u32[]{:S(2)}, u32[]{:S(2)}) %collective-permute-start.3) | collective-permute-done | bytes 36896 | tf_op jit(solution)/shard_map/ppermute | solution.py:441
  80.8 0.8 collective-permute-done.4.t2_ref
  81.5 1.3 %collective-permute-done.5.t3_ref = f32[72,128]{1,0:T(8,128)S(1)} collective-permute-done((f32[72,128]{1,0:T(8,128)S(1)}, f32[72,128]{1,0:T(8,128)S(1)}, u32[]{:S(2)}, u32[]{:S(2)}) %collective-permute-start.5) | collective-permute-done | bytes 36896 | tf_op jit(solution)/shard_map/ppermute | solution.py:441
  82.8 2.4 %recover.1 = f32[3,4,10368]{2,1,0:T(4,128)} custom-call(f32[72,128]{1,0:T(8,128)S(1)} %get-tuple-element.26.t0_ref, f32[72,128]{1,0:T(8,128)S(1)} %collective-permute-done.3.t1_ref, f32[72,128]{1,0:T(8,128)S(1)} %collective-permute-done.4.t2_ref, f32[72,128]{1,0:T(8,128)S(1)} %collective-permute-done.5.t3_ref, f32[1024,128]{1,0:T(8,128)S(1)} %bitcast.7, ...), custom_call_target="tpu_custom_call" | custom-call | tf_op jit(solution)/shard_map/recover/pallas_call | solution.py:426
  (50 shorter events, 0.2 us)
Async XLA Ops:
  2.7 14.9 %copy-start.21 = (f32[2,36,81]{2,0,1:T(2,128)S(1)}, f32[2,36,81]{2,0,1:T(2,128)}, u32[]{:S(2)}) copy-start(f32[2,36,81]{2,0,1:T(2,128)} %param.28) | copy-start | bytes 69988
  2.7 15.0 %copy-start.22 = (f32[2,81,36]{1,0,2:T(2,128)S(1)}, f32[2,81,36]{1,0,2:T(2,128)}, u32[]{:S(2)}) copy-start(f32[2,81,36]{1,0,2:T(2,128)} %param.29) | copy-start | bytes 69988
  2.7 15.1 %copy-start.11 = (f32[256,81]{1,0:T(8,128)S(1)}, f32[256,81]{1,0:T(8,128)}, u32[]{:S(2)}) copy-start(f32[256,81]{1,0:T(8,128)} %constant.25.clone.node_ref) | copy-start | bytes 248836
  2.7 15.1 %copy-start.12 = (f32[128,256]{1,0:T(8,128)S(1)}, f32[128,256]{1,0:T(8,128)}, u32[]{:S(2)}) copy-start(f32[128,256]{1,0:T(8,128)} %constant.26.clone.mrn_ref) | copy-start | bytes 393220
  2.7 15.1 %copy-start.13 = (f32[128,36]{1,0:T(8,128)S(1)}, f32[128,36]{1,0:T(8,128)}, u32[]{:S(2)}) copy-start(f32[128,36]{1,0:T(8,128)} %constant.24.clone.edge_ref) | copy-start | bytes 55300
  2.7 15.1 %copy-start.14 = (f32[128,128]{1,0:T(8,128)S(1)}, f32[128,128]{1,0:T(8,128)}, u32[]{:S(2)}) copy-start(f32[128,128]{1,0:T(8,128)} %constant.27.clone.mrr_ref) | copy-start | bytes 196612
  2.7 15.1 %copy-start.15 = (f32[128,128]{1,0:T(8,128)S(1)}, f32[128,128]{1,0:T(8,128)}, u32[]{:S(2)}) copy-start(f32[128,128]{1,0:T(8,128)} %constant.28.clone.perm_ref) | copy-start | bytes 196612
  2.8 31.4 %copy-start.9 = (bf16[256,256]{1,0:T(8,128)(2,1)S(1)}, bf16[256,256]{1,0:T(8,128)(2,1)}, u32[]{:S(2)}) copy-start(bf16[256,256]{1,0:T(8,128)(2,1)} %constant.33.clone.ah_ref) | copy-start | bytes 393220
  2.8 31.4 %copy-start.10 = (bf16[256,256]{1,0:T(8,128)(2,1)S(1)}, bf16[256,256]{1,0:T(8,128)(2,1)}, u32[]{:S(2)}) copy-start(bf16[256,256]{1,0:T(8,128)(2,1)} %constant.34.clone.al_ref) | copy-start | bytes 393220
  2.8 31.4 %all-to-all-start = ((f32[64,16,128]{2,1,0:T(8,128)}), f32[64,16,128]{2,1,0:T(8,128)S(1)}, u32[]{:S(2)}, u32[]{:S(2)}) async-start(f32[64,16,128]{2,1,0:T(8,128)} %bitcast.12), calls=%async_computation | async-start | bytes 1048576 | tf_op jit(solution)/shard_map/all_to_all | solution.py:437
  17.6 16.6 %copy-start.3 = (bf16[256,512]{1,0:T(8,128)(2,1)S(1)}, bf16[256,512]{1,0:T(8,128)(2,1)}, u32[]{:S(2)}) copy-start(bf16[256,512]{1,0:T(8,128)(2,1)} %constant.32.clone.dl_ref) | copy-start | bytes 786436
  18.5 15.7 %copy-start = (bf16[512,256]{1,0:T(8,128)(2,1)S(1)}, bf16[512,256]{1,0:T(8,128)(2,1)}, u32[]{:S(2)}) copy-start(bf16[512,256]{1,0:T(8,128)(2,1)} %constant.29.clone.th_ref) | copy-start | bytes 786436
  18.5 15.7 %copy-start.1 = (bf16[512,256]{1,0:T(8,128)(2,1)S(1)}, bf16[512,256]{1,0:T(8,128)(2,1)}, u32[]{:S(2)}) copy-start(bf16[512,256]{1,0:T(8,128)(2,1)} %constant.30.clone.tl_ref) | copy-start | bytes 786436
  18.5 15.7 %copy-start.2 = (bf16[256,512]{1,0:T(8,128)(2,1)S(1)}, bf16[256,512]{1,0:T(8,128)(2,1)}, u32[]{:S(2)}) copy-start(bf16[256,512]{1,0:T(8,128)(2,1)} %constant.31.clone.dh_ref) | copy-start | bytes 786436
  20.0 16.4 %copy-start.4 = (f32[256,256]{1,0:T(8,128)}, f32[256,256]{1,0:T(8,128)S(1)}, u32[]{:S(2)}) copy-start(f32[256,256]{1,0:T(8,128)S(1)} %get-tuple-element.19.lift_ref) | copy-start | bytes 786436
  20.0 16.4 %copy-start.6 = (f32[256,256]{1,0:T(8,128)}, f32[256,256]{1,0:T(8,128)S(1)}, u32[]{:S(2)}) copy-start(f32[256,256]{1,0:T(8,128)S(1)} %get-tuple-element.30.rec_ref) | copy-start | bytes 786436
  36.4 21.0 %copy-start.5 = (f32[256,256]{1,0:T(8,128)S(1)}, f32[256,256]{1,0:T(8,128)}, u32[]{:S(2)}) copy-start(f32[256,256]{1,0:T(8,128)} %copy-done.4) | copy-start | bytes 786436
  58.1 24.7 %copy-start.7 = (f32[256,256]{1,0:T(8,128)S(1)}, f32[256,256]{1,0:T(8,128)}, u32[]{:S(2)}) copy-start(f32[256,256]{1,0:T(8,128)} %copy-done.6) | copy-start | bytes 786436
  58.1 11.2 %collective-permute-start = (f32[96,128]{1,0:T(8,128)S(1)}, f32[96,128]{1,0:T(8,128)S(1)}, u32[]{:S(2)}, u32[]{:S(2)}) collective-permute-start(f32[96,128]{1,0:T(8,128)S(1)} %get-tuple-element.22), channel_id=1, source_target_pairs={{0,1},{1,2},{2,3},{3,0},{4,5},{5,6},{6,7},{7,4},{8,9},{9,10},{10,1... | collective-permute-start | bytes 147464 | tf_op jit(solution)/shard_map/ppermute | solution.py:441
  66.1 5.8 %collective-permute-start.1 = (f32[96,128]{1,0:T(8,128)S(1)}, f32[96,128]{1,0:T(8,128)S(1)}, u32[]{:S(2)}, u32[]{:S(2)}) collective-permute-start(f32[96,128]{1,0:T(8,128)S(1)} %get-tuple-element.23), channel_id=1, source_target_pairs={{0,2},{1,3},{2,0},{3,1},{4,6},{5,7},{6,4},{7,5},{8,10},{9,11},{10,... | collective-permute-start | bytes 147464 | tf_op jit(solution)/shard_map/ppermute | solution.py:441
  66.5 5.4 %collective-permute-start.2 = (f32[96,128]{1,0:T(8,128)S(1)}, f32[96,128]{1,0:T(8,128)S(1)}, u32[]{:S(2)}, u32[]{:S(2)}) collective-permute-start(f32[96,128]{1,0:T(8,128)S(1)} %get-tuple-element.24), channel_id=1, source_target_pairs={{0,3},{1,0},{2,1},{3,2},{4,7},{5,4},{6,5},{7,6},{8,11},{9,8},{10,9... | collective-permute-start | bytes 147464 | tf_op jit(solution)/shard_map/ppermute | solution.py:441
  74.9 5.9 %collective-permute-start.3 = (f32[72,128]{1,0:T(8,128)S(1)}, f32[72,128]{1,0:T(8,128)S(1)}, u32[]{:S(2)}, u32[]{:S(2)}) collective-permute-start(f32[72,128]{1,0:T(8,128)S(1)} %get-tuple-element.27), channel_id=1, source_target_pairs={{0,1},{1,2},{2,3},{3,0},{4,5},{5,6},{6,7},{7,4},{8,9},{9,10},{10,1... | collective-permute-start | bytes 110600 | tf_op jit(solution)/shard_map/ppermute | solution.py:441
  76.1 5.5 %collective-permute-start.4 = (f32[72,128]{1,0:T(8,128)S(1)}, f32[72,128]{1,0:T(8,128)S(1)}, u32[]{:S(2)}, u32[]{:S(2)}) collective-permute-start(f32[72,128]{1,0:T(8,128)S(1)} %get-tuple-element.28), channel_id=1, source_target_pairs={{0,2},{1,3},{2,0},{3,1},{4,6},{5,7},{6,4},{7,5},{8,10},{9,11},{10,... | collective-permute-start | bytes 110600 | tf_op jit(solution)/shard_map/ppermute | solution.py:441
  78.9 4.0 %collective-permute-start.5 = (f32[72,128]{1,0:T(8,128)S(1)}, f32[72,128]{1,0:T(8,128)S(1)}, u32[]{:S(2)}, u32[]{:S(2)}) collective-permute-start(f32[72,128]{1,0:T(8,128)S(1)} %get-tuple-element.29), channel_id=1, source_target_pairs={{0,3},{1,0},{2,1},{3,2},{4,7},{5,4},{6,5},{7,6},{8,11},{9,8},{10,9... | collective-permute-start | bytes 110600 | tf_op jit(solution)/shard_map/ppermute | solution.py:441
  (7 other events, 61.8 us)

commit v3 on v2

--- a/solution.py
+++ b/solution.py
@@ -87,7 +87,7 @@
     for p in range(GROUPS):
         for el in range(2):
             perm[2 * p + el, el * GROUPS + p] = 1
-    pick = np.zeros((64, 24), np.float32)
+    pick = np.zeros((64, 24), ml_dtypes.bfloat16)
     for c in range(3):
         for k in range(QUAD):
             pick[c * QUAD + k, 2 + k] = 1
@@ -112,51 +112,63 @@
 NT = (((1,), (1,)), ((), ()))
 
 
-PACK_STEPS = 2
-PACK_ELEMS = 2 * GROUPS // PACK_STEPS
+PACK_IN = (16, 48, 128)
+PACK_OUT = (40, 80, 112, 128)
 
 
 def window_base(e):
     return min(NODE * e // 128 * 128, PART_NODES - 256)
 
 
-PACK_CUTS = (0,) + tuple(window_base(PACK_ELEMS * (g + 1) - 1) + 256 for g in range(PACK_STEPS))
-
-
 def pack_kernel(v_ref, o_ref, v_scr, o_scr, in_sems, out_sems):
     lane = lax.broadcasted_iota(jnp.int32, (4, 256), 1)
+    col_cuts = [0] + [window_base(e - 1) + 256 for e in PACK_IN]
+    row_cuts = [0] + [8 * e for e in PACK_OUT]
 
     def arriving(g):
-        cols = slice(PACK_CUTS[g], PACK_CUTS[g + 1])
+        cols = slice(col_cuts[g], col_cuts[g + 1])
         return pltpu.make_async_copy(v_ref.at[:, :, cols], v_scr.at[:, :, cols], in_sems.at[g])
 
     def leaving(g):
-        rows = slice(8 * PACK_ELEMS * g, 8 * PACK_ELEMS * (g + 1))
+        rows = slice(row_cuts[g], row_cuts[g + 1])
         return pltpu.make_async_copy(o_scr.at[rows], o_ref.at[rows], out_sems.at[g])
 
-    for g in range(PACK_STEPS):
+    for g in range(len(PACK_IN)):
         arriving(g).start()
-    for g in range(PACK_STEPS):
-        arriving(g).wait()
-        for e in range(PACK_ELEMS * g, PACK_ELEMS * (g + 1)):
-            start = NODE * e
-            base = window_base(e)
-            rows = jnp.zeros((4, 256), F32)
-            for c in range(3):
-                window = v_scr[c, :, base:base + 256]
-                turned = pltpu.roll(window, (NODE * c - (start - base)) % 256, 1)
-                rows = jnp.where((lane >= NODE * c) & (lane < NODE * (c + 1)), turned, rows)
-            at = 16 * (e // 2) + 4 * (e % 2)
-            o_scr[at:at + 4, :] = rows[:, :128]
-            o_scr[at + 8:at + 12, :] = rows[:, 128:]
-        leaving(g).start()
-    for g in range(PACK_STEPS):
+    def piece(e, c):
+        base = window_base(e)
+        return v_scr[c, :, base:base + 128], v_scr[c, :, base + 128:base + 256], (NODE * c - (NODE * e - base)) % 256
+
+    half_row = lax.broadcasted_iota(jnp.int32, (8, 256), 0) >> 2
+    both_lane = lax.broadcasted_iota(jnp.int32, (8, 256), 1) - NODE * half_row
+    for e in range(0, 2 * GROUPS, 2):
+        if e in (0,) + PACK_IN[:-1]:
+            arriving(((0,) + PACK_IN).index(e)).wait()
+        rows = jnp.zeros((8, 256), F32)
+        for c in range(2):
+            low, high, shift = piece(e, c)
+            other = piece(e + 1, c + 1)
+            swap = (other[2] - shift) % 256 != 0
+            window = jnp.concatenate([jnp.concatenate([low, other[int(swap)]], axis=0),
+                                      jnp.concatenate([high, other[1 - int(swap)]], axis=0)], axis=1)
+            rows = jnp.where((both_lane >= NODE * c) & (both_lane < NODE * (c + 1)), pltpu.roll(window, shift, 1), rows)
+        low, high, shift = piece(e, 2)
+        third = pltpu.roll(jnp.concatenate([low, high], axis=1), shift, 1)
+        low, high, shift = piece(e + 1, 0)
+        first = pltpu.roll(jnp.concatenate([low, high], axis=1), shift, 1)
+        rest = jnp.concatenate([jnp.where(lane < 3 * NODE, x, 0.0) for x in (third, first)], axis=0)
+        rows = jnp.where((both_lane >= 2 * NODE) | (both_lane < 0), rest, rows)
+        o_scr[8 * e:8 * e + 8, :] = rows[:, :128]
+        o_scr[8 * e + 8:8 * e + 16, :] = rows[:, 128:]
+        if e + 2 in PACK_OUT:
+            leaving(PACK_OUT.index(e + 2)).start()
+    for g in range(len(PACK_OUT)):
         leaving(g).wait()
 
 
 def prep_kernel(geo_ref, kind_ref, scale_ref, dir_ref, stiff_ref, mass_ref, lift_ref, rec_ref,
                 edge_ref, node_ref, mrn_ref, mrr_ref, perm_ref,
-                lift_out, w_out, rec_out, geo_out, aux_out, aux_scr):
+                lift_high, lift_low, w_out, rec_high, rec_low, geo_out, aux_out, aux_scr):
     place = lax.axis_index("planes")
     lane = lax.broadcasted_iota(jnp.int32, (4, 256), 1)
     for el in range(2):
@@ -173,10 +185,10 @@
     node = node_ref[...]
     for t in range(2):
         rows = slice(128 * t, 128 * (t + 1))
-        lift_out[rows, :] = dot6(dot6(edge, lift_ref[t]), node, NT) * mrn_ref[...]
-        rec_out[rows, :] = dot6(dot6(edge, rec_ref[t], NT), node, NT) * mrn_ref[...]
+        lift_high[rows, :], lift_low[rows, :] = split(dot6(dot6(edge, lift_ref[t]), node, NT) * mrn_ref[...])
+        rec_high[rows, :], rec_low[rows, :] = split(dot6(dot6(edge, rec_ref[t], NT), node, NT) * mrn_ref[...])
         mixed = stiff_ref[t] + lam * mass_ref[t]
-        w_out[:, rows] = dot6(dot6(edge, mixed), edge, NT) * mrr_ref[...]
+        w_out[:128, rows], w_out[128:, rows] = split(dot6(dot6(edge, mixed), edge, NT) * mrr_ref[...])
     second = (kind_ref[...] == 1).astype(F32)
     aux_scr[...] = jnp.zeros((24, 128), F32)
     aux_scr[0:1, :] = scale_ref[...] * (1.0 - second)
@@ -252,6 +264,17 @@
     return jnp.concatenate([turn(x, first - 16 * g) for g in range(4)], axis=0)
 
 
+def put_halo(ref, x):
+    ref[27:32] = x[0:5]
+    ref[59:62] = x[5:8]
+
+
+def get_halo(ref, scr):
+    scr[0:5] = ref[27:32]
+    scr[5:8] = ref[59:62]
+    return scr[...]
+
+
 def take_top(h):
     p, el, height = lanes(32)
     return jnp.where(height == 31, 0.0, jnp.where(el == 0, turn(h, 64), turn(h, 63)))
@@ -262,14 +285,14 @@
     return jnp.where(height == 0, 0.0, jnp.where(el == 1, turn(h, 64), turn(h, -63)))
 
 
-def lift_kernel(x_ref, lift_ref, aux_ref, o0_ref, o1_ref, o2_ref, o3_ref, in_scr, out_scr):
+def lift_kernel(x_ref, lift_high, lift_low, aux_ref, o0_ref, o1_ref, o2_ref, o3_ref, in_scr, out_scr):
     arrived = jnp.transpose(x_ref[...].reshape(GROUPS, 16, 128), (1, 0, 2))
     for q in range(4):
         for el in range(2):
             at = (2 * q + el) * 64
             for t in range(2):
                 in_scr[at:at + 64, t * 128:(t + 1) * 128] = arrived[t * 8 + el * 4 + q]
-    lifted = dot3(split(lift_ref[...]), split(in_scr[...]), NT)
+    lifted = dot3((lift_high[...], lift_low[...]), split(in_scr[...]), NT)
     second = aux_ref[20:21, :] > 0.5
     p = lanes(32)[0]
     for q in range(4):
@@ -278,13 +301,13 @@
         right = edges[32:64]
         out_scr[q, 0:32] = edges[0:32] + jnp.where(p >= 16, turn(right, 16), 0.0)
         out_scr[q, 32:64] = edges[64:96] + give_top(edges[96:128])
-        out_scr[q, 64:72] = fold(right, 48)
-        out_scr[q, 72:96] = aux_ref[...]
+        put_halo(out_scr.at[q], fold(right, 48))
+        out_scr[q, 64:88] = aux_ref[...]
     for k, ref in enumerate((o0_ref, o1_ref, o2_ref, o3_ref)):
         ref[...] = out_scr[lax.rem(lax.axis_index("elem") + k, PARTS)]
 
 
-def cg_kernel(f0_ref, f1_ref, f2_ref, f3_ref, w_ref, pick_ref, o0_ref, o1_ref, o2_ref, o3_ref, scr):
+def cg_kernel(f0_ref, f1_ref, f2_ref, f3_ref, w_ref, pick_ref, o0_ref, o1_ref, o2_ref, o3_ref, scr, halo_scr):
     for k, ref in enumerate((f0_ref, f1_ref, f2_ref, f3_ref)):
         scr[lax.rem(lax.axis_index("elem") + PARTS - k, PARTS)] = ref[...]
     p = lanes(32)[0]
@@ -315,12 +338,12 @@
         v, h = x[:32], x[32:]
         return jnp.concatenate([v, right_of(v), h, top_of(h)], axis=0)
 
-    aux = jnp.concatenate([scr[i, 72:96] for i in range(PARTS)], axis=1)
-    free = dot6(pick_ref[...], aux)
+    aux = jnp.concatenate([scr[i, 64:88] for i in range(PARTS)], axis=1)
+    free = lax.dot(pick_ref[...], aux.astype(BF16), preferred_element_type=F32)
     first_scale = aux[0:1]
     second_scale = aux[1:2]
-    w_high, w_low = split(w_ref[...])
-    w_both = jnp.concatenate([w_high, w_low], axis=0)
+    w_both = w_ref[...]
+    w_high = w_both[:128]
 
     def operator(x):
         high, low = split(x)
@@ -339,7 +362,7 @@
     for i in range(PARTS):
         v = scr[i, 0:32]
         if i > 0:
-            v = v + jnp.where(p < 16, unfold(scr[i - 1, 64:72], 0), 0.0)
+            v = v + jnp.where(p < 16, unfold(get_halo(scr.at[i - 1], halo_scr.at[i - 1]), 0), 0.0)
         sent.append(jnp.concatenate([v, scr[i, 32:64]], axis=0))
     residual = jnp.concatenate(sent, axis=1) * free
     direction = residual
@@ -358,14 +381,14 @@
     pieces = parts(trace)
     for i in range(PARTS):
         scr[i, 0:64] = pieces[i]
-        scr[i, 64:72] = fold(pieces[i + 1][:32], 0) if i < 3 else jnp.zeros((8, 128), F32)
+        put_halo(scr.at[i], fold(pieces[i + 1][:32], 0) if i < 3 else jnp.zeros((8, 128), F32))
     for k, ref in enumerate((o0_ref, o1_ref, o2_ref, o3_ref)):
-        ref[...] = scr[lax.rem(lax.axis_index("elem") + k, PARTS), 0:72]
-
-
-def recover_kernel(t0_ref, t1_ref, t2_ref, t3_ref, x_ref, rec_ref, aux_ref, o_ref, scr, t_scr, o_scr, sems):
+        ref[...] = scr[lax.rem(lax.axis_index("elem") + k, PARTS), 0:64]
+
+
+def recover_kernel(t0_ref, t1_ref, t2_ref, t3_ref, x_ref, rec_high, rec_low, aux_ref, o_ref, scr, t_scr, o_scr, halo_scr, sems):
     for k, ref in enumerate((t0_ref, t1_ref, t2_ref, t3_ref)):
-        t_scr[lax.rem(lax.axis_index("elem") + PARTS - k, PARTS), 0:72] = ref[...]
+        t_scr[lax.rem(lax.axis_index("elem") + PARTS - k, PARTS), 0:64] = ref[...]
     second = aux_ref[20:21, :]
     p = lanes(32)[0]
     row = lax.broadcasted_iota(jnp.int32, (32, 128), 0)
@@ -373,11 +396,11 @@
     for q in range(4):
         v = t_scr[q, 0:32]
         h = t_scr[q, 32:64]
-        right = jnp.where(p < 48, turn(v, -16), unfold(t_scr[q, 64:72], 48))
+        right = jnp.where(p < 48, turn(v, -16), unfold(get_halo(t_scr.at[q], halo_scr.at[q]), 48))
         vectors.append(jnp.concatenate([v, right, h, jnp.where(row == 31, second, take_top(h))], axis=0))
     turned = jnp.concatenate(vectors, axis=1).T
     kind = turned[:, 127:128]
-    recovered = dot3(split(jnp.concatenate([turned * (1.0 - kind), turned * kind], axis=1)), split(rec_ref[...]))
+    recovered = dot3(split(jnp.concatenate([turned * (1.0 - kind), turned * kind], axis=1)), (rec_high[...], rec_low[...]))
     wave = lax.div(4 * lax.axis_index("planes") + (lax.broadcasted_iota(jnp.int32, (8, 128), 0) & 3) + 1, 2).astype(F32)
     weight = 1.0 / (2.0 + (BETA_COEF * wave) * (BETA_COEF * wave))
     for t in range(2):
@@ -387,8 +410,11 @@
             scr[512 * t + 8 * g:512 * t + 8 * g + 8, :] = x_ref[16 * g + 8 * t:16 * g + 8 * t + 8, :] * weight + mine[g]
     lane = lax.broadcasted_iota(jnp.int32, (4, 128), 1)
 
-    def leaving(c):
-        return pltpu.make_async_copy(o_scr.at[c], o_ref.at[c], sems.at[c])
+    cuts = (0, 5376, PART_NODES)
+
+    def leaving(c, part):
+        cols = slice(cuts[part], cuts[part + 1])
+        return pltpu.make_async_copy(o_scr.at[c, :, cols], o_ref.at[c, :, cols], sems.at[2 * c + part])
 
     for c in range(3):
         current = jnp.zeros((4, 128), F32)
@@ -400,9 +426,11 @@
             if offset + NODE >= 128:
                 o_scr[c, :, 128 * tile:128 * (tile + 1)] = current
                 current = turned[:, 128:]
-        leaving(c).start()
+                if 128 * (tile + 1) in cuts:
+                    leaving(c, cuts.index(128 * (tile + 1)) - 1).start()
     for c in range(3):
-        leaving(c).wait()
+        for part in range(2):
+            leaving(c, part).wait()
 
 
 VMEM = pl.BlockSpec(memory_space=pltpu.VMEM)
@@ -413,6 +441,10 @@
 
 
 ANY = pl.BlockSpec(memory_space=pl.ANY)
+
+
+def half(*dims):
+    return jax.ShapeDtypeStruct(dims, BF16)
 
 
 def call(kernel, name, out, args, scratch=(), sems=(), far_in=False, far_out=False):
@@ -420,7 +452,7 @@
     if not far_in:
         args = tuple(pltpu.with_memory_space_constraint(jnp.asarray(a), pltpu.VMEM) for a in args)
     if not far_out:
-        outs = tuple(pltpu.VMEM(o.shape, F32) for o in (out if many else (out,)))
+        outs = tuple(pltpu.VMEM(o.shape, o.dtype) for o in (out if many else (out,)))
         out = outs if many else outs[0]
     place = ANY if far_out else VMEM
     return pl.pallas_call(
@@ -445,23 +477,23 @@
 def per_device(velocity, geometry, element_kind, element_scale, dirichlet, schur_stiffness, schur_mass, lift, recover):
     edge, node, mask_rn, mask_rr, perm, pick = selections()
     packed = call(pack_kernel, "pack", shape(1024, 128), (velocity,),
-                  scratch=((3, 4, PART_NODES), (1024, 128)), sems=(PACK_STEPS, PACK_STEPS), far_in=True, far_out=True)
+                  scratch=((3, 4, PART_NODES), (1024, 128)), sems=(len(PACK_IN), len(PACK_OUT)), far_in=True, far_out=True)
     arrived = exchange(packed, "planes", GROUPS).reshape(1024, 128)
-    lift_all, w_all, rec_all, geo, aux = call(
+    lift_high, lift_low, w_all, rec_high, rec_low, geo, aux = call(
         prep_kernel, "prep",
-        (shape(256, 256), shape(128, 256), shape(256, 256), shape(8, 256), shape(24, 128)),
+        (half(256, 256), half(256, 256), half(256, 256), half(256, 256), half(256, 256), shape(8, 256), shape(24, 128)),
         (geometry, element_kind.reshape(1, 128), element_scale.reshape(1, 128), dirichlet,
          schur_stiffness, schur_mass, lift, recover, edge, node, mask_rn, mask_rr, perm),
         scratch=((24, 128),))
     inter = call(advect_kernel, "advect", shape(1024, 128), (arrived,) + tables() + (geo,),
                  scratch=((512, 256), (512, 256), (256, 256)))
     owned = exchange(inter, "planes", GROUPS).reshape(1024, 128)
-    lifted = call(lift_kernel, "lift", (shape(96, 128),) * PARTS, (owned, lift_all, aux),
-                  scratch=((512, 256), (PARTS, 96, 128)))
-    traces = call(cg_kernel, "cg", (shape(72, 128),) * PARTS, spread(lifted) + (w_all, pick),
-                  scratch=((PARTS, 96, 128),))
-    return call(recover_kernel, "recover", shape(3, 4, PART_NODES), spread(traces) + (owned, rec_all, aux),
-                scratch=((1024, 128), (PARTS, 96, 128), (3, 4, PART_NODES)), sems=(3,), far_out=True)
+    lifted = call(lift_kernel, "lift", (shape(88, 128),) * PARTS, (owned, lift_high, lift_low, aux),
+                  scratch=((512, 256), (PARTS, 88, 128)))
+    traces = call(cg_kernel, "cg", (shape(64, 128),) * PARTS, spread(lifted) + (w_all, pick),
+                  scratch=((PARTS, 88, 128), (PARTS, 8, 128)))
+    return call(recover_kernel, "recover", shape(3, 4, PART_NODES), spread(traces) + (owned, rec_high, rec_low, aux),
+                scratch=((1024, 128), (PARTS, 88, 128), (3, 4, PART_NODES), (PARTS, 8, 128)), sems=(6,), far_out=True)
 
 
 def solution(mesh):

time: 85.6 us -> 85.1 us (level)
  no operation moved by 1% of the time
where the time goes in v3:
time: 85.1 us; the launch traced here: 84.7 us
  starting transfers between devices  30.3 us (36%)
  blocking collectives  21 us (25%)
  waiting for transfers between devices  20.1 us (24%)
  Pallas kernels  11.9 us (14%)
  local copies, waits for them, and re-layouts  0.94 us (1%)
    all_to_all x1, blocking collectives, exchange(): lax.all_to_all(value.reshape(count, -1, 128), axis, split_axis=0, concat_...  21 us
    ppermute x6, starting transfers between devices, spread(): lax.ppermute(blocks[k], 'elem', [(s, (s + k) % PARTS) for s in range(PART...  15.5 us
    all_to_all x1, starting transfers between devices, exchange(): lax.all_to_all(value.reshape(count, -1, 128), axis, split_axis=0, concat_...  14.7 us
    all_to_all x1, waiting for transfers between devices, exchange(): lax.all_to_all(value.reshape(count, -1, 128), axis, split_axis=0, concat_...  14.1 us
    pallas_call x6, Pallas kernels, call(): pl.pallas_call(kernel, name=name, out_shape=out, in_specs=[ANY if far_in...  11.9 us
    ppermute x6, waiting for transfers between devices, spread(): lax.ppermute(blocks[k], 'elem', [(s, (s + k) % PARTS) for s in range(PART...  6.04 us
  transfers between devices with their start and end apart: 7, of which 5 were waited for; matrix products, arithmetic and copies ran while one was open for 0% of the time, Pallas kernels for 2%

profile of v3, /device:TPU:8, one launch (start us, length us, event | category | flops | bytes accessed | tf_op | source)
XLA Modules:
  0.0 84.7 jit_solution(9612907578891878686)
XLA Ops:
  0.0 2.3 %pack.1 = f32[1024,128]{1,0:T(8,128)} custom-call(f32[3,4,10368]{2,1,0:T(4,128)} %v_ref.1), custom_call_target="tpu_custom_call" | custom-call | tf_op jit(solution)/shard_map/pack/pallas_call | solution.py:458
  2.4 0.0 copy-start.12
  2.4 0.0 copy-start.17
  2.4 0.0 copy-start.18
  2.5 14.7 %all-to-all-start = ((f32[64,16,128]{2,1,0:T(8,128)}), f32[64,16,128]{2,1,0:T(8,128)S(1)}, u32[]{:S(2)}, u32[]{:S(2)}) async-start(f32[64,16,128]{2,1,0:T(8,128)} %bitcast.12), calls=%async_computation | async-start | bytes 1048576 | tf_op jit(solution)/shard_map/all_to_all | solution.py:469
  17.3 0.1 copy.26.rec_ref
  17.5 0.6 copy-done.4
  18.2 1.5 %prep.1 = (bf16[256,256]{1,0:T(8,128)(2,1)S(1)}, bf16[256,256]{1,0:T(8,128)(2,1)S(1)}, bf16[256,256]{1,0:T(8,128)(2,1)S(1)}, bf16[256,256]{1,0:T(8,128)(2,1)S(1)...) custom-call(f32[4,10368]{1,0:T(4,128)S(1)} %copy-done.4, s32[1,128]{1,0:T(1,128)S(1)} %bitcast.10, ...), custom_call_target="tpu_custom_call" | custom-call | tf_op jit(solution)/shard_map/prep/pallas_call | solution.py:458
  19.7 14.1 %all-to-all-done = f32[64,16,128]{2,1,0:T(8,128)S(1)} async-done(((f32[64,16,128]{2,1,0:T(8,128)}), f32[64,16,128]{2,1,0:T(8,128)S(1)}, u32[]{:S(2)}, u32[]{:S(2)}) %all-to-all-start) | async-done | bytes 524320 | tf_op jit(solution)/shard_map/all_to_all | solution.py:469
  33.9 2.2 %advect.1 = f32[1024,128]{1,0:T(8,128)S(1)} custom-call(f32[1024,128]{1,0:T(8,128)S(1)} %bitcast.8, bf16[512,256]{1,0:T(8,128)(2,1)S(1)} %copy-done, bf16[512,256]{1,0:T(8,128)(2,1)S(1)} %copy-done.1, bf16[256,512]{1,0:T(8,128)(2,1)S(1)} %copy-done.2, bf16[256,512]{1,0:T(8,128)(2,1)S(1)} %copy-done.3, bf16[256,256]{1,0:T(8,128)(2,1)S(1)} %copy-done.5, ...), custom_call_target="tpu_custom_call" | custom-call | tf_op jit(solution)/shard_map/advect/pallas_call | solution.py:458
  36.2 21.0 %all_to_all.10 = f32[64,16,128]{2,1,0:T(8,128)S(1)} all-to-all(f32[64,16,128]{2,1,0:T(8,128)S(1)} %bitcast.9), channel_id=1, replica_groups=mesh['planes'=64,'elem'=4] {'planes'}, dimensions={0} | all-to-all | bytes 1048576 | tf_op jit(solution)/shard_map/all_to_all | solution.py:469
  57.2 0.6 lift.1
  57.8 8.0 %collective-permute-start = (f32[88,128]{1,0:T(8,128)S(1)}, f32[88,128]{1,0:T(8,128)S(1)}, u32[]{:S(2)}, u32[]{:S(2)}) collective-permute-start(f32[88,128]{1,0:T(8,128)S(1)} %get-tuple-element.25), channel_id=1, source_target_pairs={{0,1},{1,2},{2,3},{3,0},{4,5},{5,6},{6,7},{7,4},{8,9},{9,10},{10,1... | collective-permute-start | bytes 135176 | tf_op jit(solution)/shard_map/ppermute | solution.py:473
  65.7 0.4 collective-permute-start.1
  66.2 2.8 %collective-permute-start.2 = (f32[88,128]{1,0:T(8,128)S(1)}, f32[88,128]{1,0:T(8,128)S(1)}, u32[]{:S(2)}, u32[]{:S(2)}) collective-permute-start(f32[88,128]{1,0:T(8,128)S(1)} %get-tuple-element.27), channel_id=1, source_target_pairs={{0,3},{1,0},{2,1},{3,2},{4,7},{5,4},{6,5},{7,6},{8,11},{9,8},{10,9... | collective-permute-start | bytes 135176 | tf_op jit(solution)/shard_map/ppermute | solution.py:473
  69.0 2.4 %collective-permute-done.1.f2_ref = f32[88,128]{1,0:T(8,128)S(1)} collective-permute-done((f32[88,128]{1,0:T(8,128)S(1)}, f32[88,128]{1,0:T(8,128)S(1)}, u32[]{:S(2)}, u32[]{:S(2)}) %collective-permute-start.1) | collective-permute-done | bytes 45088 | tf_op jit(solution)/shard_map/ppermute | solution.py:473
  71.4 2.9 %cg.1 = (f32[64,128]{1,0:T(8,128)S(1)}, f32[64,128]{1,0:T(8,128)S(1)}, f32[64,128]{1,0:T(8,128)S(1)}, f32[64,128]{1,0:T(8,128)S(1)}) custom-call(f32[88,128]{1,0:T(8,128)S(1)} %get-tuple-element.24.f0_ref, f32[88,128]{1,0:T(8,128)S(1)} %collective-permute-done.f1_ref, f32[88,128]{1,0:T(8,128)S(1)} %collective-permute-done.1.f2_ref, ...), custom_call_target="tpu_custom_call" | custom-call | tf_op jit(solution)/shard_map/cg/pallas_call | solution.py:458
  74.3 1.1 %collective-permute-start.3 = (f32[64,128]{1,0:T(8,128)S(1)}, f32[64,128]{1,0:T(8,128)S(1)}, u32[]{:S(2)}, u32[]{:S(2)}) collective-permute-start(f32[64,128]{1,0:T(8,128)S(1)} %get-tuple-element.30), channel_id=1, source_target_pairs={{0,1},{1,2},{2,3},{3,0},{4,5},{5,6},{6,7},{7,4},{8,9},{9,10},{10,1... | collective-permute-start | bytes 98312 | tf_op jit(solution)/shard_map/ppermute | solution.py:473
  75.4 3.0 %collective-permute-start.4 = (f32[64,128]{1,0:T(8,128)S(1)}, f32[64,128]{1,0:T(8,128)S(1)}, u32[]{:S(2)}, u32[]{:S(2)}) collective-permute-start(f32[64,128]{1,0:T(8,128)S(1)} %get-tuple-element.31), channel_id=1, source_target_pairs={{0,2},{1,3},{2,0},{3,1},{4,6},{5,7},{6,4},{7,5},{8,10},{9,11},{10,... | collective-permute-start | bytes 98312 | tf_op jit(solution)/shard_map/ppermute | solution.py:473
  78.4 0.2 collective-permute-start.5
  78.6 1.5 %collective-permute-done.3.t1_ref = f32[64,128]{1,0:T(8,128)S(1)} collective-permute-done((f32[64,128]{1,0:T(8,128)S(1)}, f32[64,128]{1,0:T(8,128)S(1)}, u32[]{:S(2)}, u32[]{:S(2)}) %collective-permute-start.3) | collective-permute-done | bytes 32800 | tf_op jit(solution)/shard_map/ppermute | solution.py:473
  80.1 0.7 collective-permute-done.4.t2_ref
  80.8 1.5 %collective-permute-done.5.t3_ref = f32[64,128]{1,0:T(8,128)S(1)} collective-permute-done((f32[64,128]{1,0:T(8,128)S(1)}, f32[64,128]{1,0:T(8,128)S(1)}, u32[]{:S(2)}, u32[]{:S(2)}) %collective-permute-start.5) | collective-permute-done | bytes 32800 | tf_op jit(solution)/shard_map/ppermute | solution.py:473
  82.3 2.4 %recover.1 = f32[3,4,10368]{2,1,0:T(4,128)} custom-call(f32[64,128]{1,0:T(8,128)S(1)} %get-tuple-element.29.t0_ref, f32[64,128]{1,0:T(8,128)S(1)} %collective-permute-done.3.t1_ref, f32[64,128]{1,0:T(8,128)S(1)} %collective-permute-done.4.t2_ref, f32[64,128]{1,0:T(8,128)S(1)} %collective-permute-done.5.t3_ref, f32[1024,128]{1,0:T(8,128)S(1)} %bitcast.7, ...), custom_call_target="tpu_custom_call" | custom-call | tf_op jit(solution)/shard_map/recover/pallas_call | solution.py:458
  (58 shorter events, 0.2 us)
Async XLA Ops:
  2.4 15.0 %copy-start.26 = (f32[2,81,36]{1,0,2:T(2,128)S(1)}, f32[2,81,36]{1,0,2:T(2,128)}, u32[]{:S(2)}) copy-start(f32[2,81,36]{1,0,2:T(2,128)} %param.29) | copy-start | bytes 69988
  2.4 15.1 %copy-start.11 = (f32[256,81]{1,0:T(8,128)S(1)}, f32[256,81]{1,0:T(8,128)}, u32[]{:S(2)}) copy-start(f32[256,81]{1,0:T(8,128)} %constant.25.clone.node_ref) | copy-start | bytes 248836
  2.4 15.1 %copy-start.12 = (f32[128,256]{1,0:T(8,128)S(1)}, f32[128,256]{1,0:T(8,128)}, u32[]{:S(2)}) copy-start(f32[128,256]{1,0:T(8,128)} %constant.26.clone.mrn_ref) | copy-start | bytes 393220
  2.4 15.1 %copy-start.17 = (f32[128,36]{1,0:T(8,128)S(1)}, f32[128,36]{1,0:T(8,128)}, u32[]{:S(2)}) copy-start(f32[128,36]{1,0:T(8,128)} %constant.24.clone.edge_ref) | copy-start | bytes 55300
  2.4 15.1 %copy-start.18 = (f32[128,128]{1,0:T(8,128)S(1)}, f32[128,128]{1,0:T(8,128)}, u32[]{:S(2)}) copy-start(f32[128,128]{1,0:T(8,128)} %constant.27.clone.mrr_ref) | copy-start | bytes 196612
  2.4 15.1 %copy-start.19 = (f32[128,128]{1,0:T(8,128)S(1)}, f32[128,128]{1,0:T(8,128)}, u32[]{:S(2)}) copy-start(f32[128,128]{1,0:T(8,128)} %constant.28.clone.perm_ref) | copy-start | bytes 196612
  2.4 31.4 %copy-start.5 = (bf16[256,256]{1,0:T(8,128)(2,1)S(1)}, bf16[256,256]{1,0:T(8,128)(2,1)}, u32[]{:S(2)}) copy-start(bf16[256,256]{1,0:T(8,128)(2,1)} %constant.33.clone.ah_ref) | copy-start | bytes 393220
  2.4 31.4 %copy-start.6 = (bf16[256,256]{1,0:T(8,128)(2,1)S(1)}, bf16[256,256]{1,0:T(8,128)(2,1)}, u32[]{:S(2)}) copy-start(bf16[256,256]{1,0:T(8,128)(2,1)} %constant.34.clone.al_ref) | copy-start | bytes 393220
  2.5 31.4 %all-to-all-start = ((f32[64,16,128]{2,1,0:T(8,128)}), f32[64,16,128]{2,1,0:T(8,128)S(1)}, u32[]{:S(2)}, u32[]{:S(2)}) async-start(f32[64,16,128]{2,1,0:T(8,128)} %bitcast.12), calls=%async_computation | async-start | bytes 1048576 | tf_op jit(solution)/shard_map/all_to_all | solution.py:469
  17.3 16.6 %copy-start.3 = (bf16[256,512]{1,0:T(8,128)(2,1)S(1)}, bf16[256,512]{1,0:T(8,128)(2,1)}, u32[]{:S(2)}) copy-start(bf16[256,512]{1,0:T(8,128)(2,1)} %constant.32.clone.dl_ref) | copy-start | bytes 786436
  18.1 15.7 %copy-start = (bf16[512,256]{1,0:T(8,128)(2,1)S(1)}, bf16[512,256]{1,0:T(8,128)(2,1)}, u32[]{:S(2)}) copy-start(bf16[512,256]{1,0:T(8,128)(2,1)} %constant.29.clone.th_ref) | copy-start | bytes 786436
  18.1 15.7 %copy-start.1 = (bf16[512,256]{1,0:T(8,128)(2,1)S(1)}, bf16[512,256]{1,0:T(8,128)(2,1)}, u32[]{:S(2)}) copy-start(bf16[512,256]{1,0:T(8,128)(2,1)} %constant.30.clone.tl_ref) | copy-start | bytes 786436
  18.1 15.7 %copy-start.2 = (bf16[256,512]{1,0:T(8,128)(2,1)S(1)}, bf16[256,512]{1,0:T(8,128)(2,1)}, u32[]{:S(2)}) copy-start(bf16[256,512]{1,0:T(8,128)(2,1)} %constant.31.clone.dh_ref) | copy-start | bytes 786436
  19.7 16.4 %copy-start.7 = (bf16[256,256]{1,0:T(8,128)(2,1)}, bf16[256,256]{1,0:T(8,128)(2,1)S(1)}, u32[]{:S(2)}) copy-start(bf16[256,256]{1,0:T(8,128)(2,1)S(1)} %get-tuple-element.22.lift_low) | copy-start | bytes 393220
  19.7 16.4 %copy-start.9 = (bf16[256,256]{1,0:T(8,128)(2,1)}, bf16[256,256]{1,0:T(8,128)(2,1)S(1)}, u32[]{:S(2)}) copy-start(bf16[256,256]{1,0:T(8,128)(2,1)S(1)} %get-tuple-element.28.w_ref) | copy-start | bytes 393220
  19.7 16.4 %copy-start.13 = (bf16[256,256]{1,0:T(8,128)(2,1)}, bf16[256,256]{1,0:T(8,128)(2,1)S(1)}, u32[]{:S(2)}) copy-start(bf16[256,256]{1,0:T(8,128)(2,1)S(1)} %get-tuple-element.33.rec_high) | copy-start | bytes 393220
  19.7 16.4 %copy-start.15 = (bf16[256,256]{1,0:T(8,128)(2,1)}, bf16[256,256]{1,0:T(8,128)(2,1)S(1)}, u32[]{:S(2)}) copy-start(bf16[256,256]{1,0:T(8,128)(2,1)S(1)} %get-tuple-element.34.rec_low) | copy-start | bytes 393220
  36.1 21.0 %copy-start.8 = (bf16[256,256]{1,0:T(8,128)(2,1)S(1)}, bf16[256,256]{1,0:T(8,128)(2,1)}, u32[]{:S(2)}) copy-start(bf16[256,256]{1,0:T(8,128)(2,1)} %copy-done.7) | copy-start | bytes 393220
  57.8 11.2 %collective-permute-start = (f32[88,128]{1,0:T(8,128)S(1)}, f32[88,128]{1,0:T(8,128)S(1)}, u32[]{:S(2)}, u32[]{:S(2)}) collective-permute-start(f32[88,128]{1,0:T(8,128)S(1)} %get-tuple-element.25), channel_id=1, source_target_pairs={{0,1},{1,2},{2,3},{3,0},{4,5},{5,6},{6,7},{7,4},{8,9},{9,10},{10,1... | collective-permute-start | bytes 135176 | tf_op jit(solution)/shard_map/ppermute | solution.py:473
  65.7 5.6 %collective-permute-start.1 = (f32[88,128]{1,0:T(8,128)S(1)}, f32[88,128]{1,0:T(8,128)S(1)}, u32[]{:S(2)}, u32[]{:S(2)}) collective-permute-start(f32[88,128]{1,0:T(8,128)S(1)} %get-tuple-element.26), channel_id=1, source_target_pairs={{0,2},{1,3},{2,0},{3,1},{4,6},{5,7},{6,4},{7,5},{8,10},{9,11},{10,... | collective-permute-start | bytes 135176 | tf_op jit(solution)/shard_map/ppermute | solution.py:473
  66.2 5.2 %collective-permute-start.2 = (f32[88,128]{1,0:T(8,128)S(1)}, f32[88,128]{1,0:T(8,128)S(1)}, u32[]{:S(2)}, u32[]{:S(2)}) collective-permute-start(f32[88,128]{1,0:T(8,128)S(1)} %get-tuple-element.27), channel_id=1, source_target_pairs={{0,3},{1,0},{2,1},{3,2},{4,7},{5,4},{6,5},{7,6},{8,11},{9,8},{10,9... | collective-permute-start | bytes 135176 | tf_op jit(solution)/shard_map/ppermute | solution.py:473
  74.3 5.8 %collective-permute-start.3 = (f32[64,128]{1,0:T(8,128)S(1)}, f32[64,128]{1,0:T(8,128)S(1)}, u32[]{:S(2)}, u32[]{:S(2)}) collective-permute-start(f32[64,128]{1,0:T(8,128)S(1)} %get-tuple-element.30), channel_id=1, source_target_pairs={{0,1},{1,2},{2,3},{3,0},{4,5},{5,6},{6,7},{7,4},{8,9},{9,10},{10,1... | collective-permute-start | bytes 98312 | tf_op jit(solution)/shard_map/ppermute | solution.py:473
  75.4 5.4 %collective-permute-start.4 = (f32[64,128]{1,0:T(8,128)S(1)}, f32[64,128]{1,0:T(8,128)S(1)}, u32[]{:S(2)}, u32[]{:S(2)}) collective-permute-start(f32[64,128]{1,0:T(8,128)S(1)} %get-tuple-element.31), channel_id=1, source_target_pairs={{0,2},{1,3},{2,0},{3,1},{4,6},{5,7},{6,4},{7,5},{8,10},{9,11},{10,... | collective-permute-start | bytes 98312 | tf_op jit(solution)/shard_map/ppermute | solution.py:473
  78.4 3.9 %collective-permute-start.5 = (f32[64,128]{1,0:T(8,128)S(1)}, f32[64,128]{1,0:T(8,128)S(1)}, u32[]{:S(2)}, u32[]{:S(2)}) collective-permute-start(f32[64,128]{1,0:T(8,128)S(1)} %get-tuple-element.32), channel_id=1, source_target_pairs={{0,3},{1,0},{2,1},{3,2},{4,7},{5,4},{6,5},{7,6},{8,11},{9,8},{10,9... | collective-permute-start | bytes 98312 | tf_op jit(solution)/shard_map/ppermute | solution.py:473
  (11 other events, 112.6 us)

commit v4 on v3

--- a/solution.py
+++ b/solution.py
@@ -113,7 +113,7 @@
 
 
 PACK_IN = (16, 48, 128)
-PACK_OUT = (40, 80, 112, 128)
+PACK_OUT = (48, 96, 120, 128)
 
 
 def window_base(e):
@@ -410,11 +410,11 @@
             scr[512 * t + 8 * g:512 * t + 8 * g + 8, :] = x_ref[16 * g + 8 * t:16 * g + 8 * t + 8, :] * weight + mine[g]
     lane = lax.broadcasted_iota(jnp.int32, (4, 128), 1)
 
-    cuts = (0, 5376, PART_NODES)
+    cuts = (0, 5376, 8960, PART_NODES)
 
     def leaving(c, part):
         cols = slice(cuts[part], cuts[part + 1])
-        return pltpu.make_async_copy(o_scr.at[c, :, cols], o_ref.at[c, :, cols], sems.at[2 * c + part])
+        return pltpu.make_async_copy(o_scr.at[c, :, cols], o_ref.at[c, :, cols], sems.at[3 * c + part])
 
     for c in range(3):
         current = jnp.zeros((4, 128), F32)
@@ -429,7 +429,7 @@
                 if 128 * (tile + 1) in cuts:
                     leaving(c, cuts.index(128 * (tile + 1)) - 1).start()
     for c in range(3):
-        for part in range(2):
+        for part in range(3):
             leaving(c, part).wait()
 
 
@@ -493,7 +493,7 @@
     traces = call(cg_kernel, "cg", (shape(64, 128),) * PARTS, spread(lifted) + (w_all, pick),
                   scratch=((PARTS, 88, 128), (PARTS, 8, 128)))
     return call(recover_kernel, "recover", shape(3, 4, PART_NODES), spread(traces) + (owned, rec_high, rec_low, aux),
-                scratch=((1024, 128), (PARTS, 88, 128), (3, 4, PART_NODES), (PARTS, 8, 128)), sems=(6,), far_out=True)
+                scratch=((1024, 128), (PARTS, 88, 128), (3, 4, PART_NODES), (PARTS, 8, 128)), sems=(9,), far_out=True)
 
 
 def solution(mesh):

time: 85.1 us -> 85.1 us (level)
  no operation moved by 1% of the time
where the time goes in v4:
time: 85.1 us; the launch traced here: 84.7 us
  starting transfers between devices  30.3 us (36%)
  blocking collectives  21 us (25%)
  waiting for transfers between devices  20.1 us (24%)
  Pallas kernels  11.9 us (14%)
  local copies, waits for them, and re-layouts  0.94 us (1%)
    all_to_all x1, blocking collectives, exchange(): lax.all_to_all(value.reshape(count, -1, 128), axis, split_axis=0, concat_...  21 us
    ppermute x6, starting transfers between devices, spread(): lax.ppermute(blocks[k], 'elem', [(s, (s + k) % PARTS) for s in range(PART...  15.5 us
    all_to_all x1, starting transfers between devices, exchange(): lax.all_to_all(value.reshape(count, -1, 128), axis, split_axis=0, concat_...  14.7 us
    all_to_all x1, waiting for transfers between devices, exchange(): lax.all_to_all(value.reshape(count, -1, 128), axis, split_axis=0, concat_...  14.1 us
    pallas_call x6, Pallas kernels, call(): pl.pallas_call(kernel, name=name, out_shape=out, in_specs=[ANY if far_in...  11.9 us
    ppermute x6, waiting for transfers between devices, spread(): lax.ppermute(blocks[k], 'elem', [(s, (s + k) % PARTS) for s in range(PART...  6.04 us
  transfers between devices with their start and end apart: 7, of which 5 were waited for; matrix products, arithmetic and copies ran while one was open for 0% of the time, Pallas kernels for 2%

profile of v4, /device:TPU:8, one launch (start us, length us, event | category | flops | bytes accessed | tf_op | source)
XLA Modules:
  0.0 84.7 jit_solution(2534291269254849252)
XLA Ops:
  0.0 2.3 %pack.1 = f32[1024,128]{1,0:T(8,128)} custom-call(f32[3,4,10368]{2,1,0:T(4,128)} %v_ref.1), custom_call_target="tpu_custom_call" | custom-call | tf_op jit(solution)/shard_map/pack/pallas_call | solution.py:458
  2.4 0.0 copy-start.11
  2.4 0.0 copy-start.17
  2.4 0.0 copy-start.18
  2.5 14.7 %all-to-all-start = ((f32[64,16,128]{2,1,0:T(8,128)}), f32[64,16,128]{2,1,0:T(8,128)S(1)}, u32[]{:S(2)}, u32[]{:S(2)}) async-start(f32[64,16,128]{2,1,0:T(8,128)} %bitcast.12), calls=%async_computation | async-start | bytes 1048576 | tf_op jit(solution)/shard_map/all_to_all | solution.py:469
  17.3 0.1 copy.26.rec_ref
  17.5 0.6 copy-done.4
  18.2 1.5 %prep.1 = (bf16[256,256]{1,0:T(8,128)(2,1)S(1)}, bf16[256,256]{1,0:T(8,128)(2,1)S(1)}, bf16[256,256]{1,0:T(8,128)(2,1)S(1)}, bf16[256,256]{1,0:T(8,128)(2,1)S(1)...) custom-call(f32[4,10368]{1,0:T(4,128)S(1)} %copy-done.4, s32[1,128]{1,0:T(1,128)S(1)} %bitcast.10, ...), custom_call_target="tpu_custom_call" | custom-call | tf_op jit(solution)/shard_map/prep/pallas_call | solution.py:458
  19.8 14.1 %all-to-all-done = f32[64,16,128]{2,1,0:T(8,128)S(1)} async-done(((f32[64,16,128]{2,1,0:T(8,128)}), f32[64,16,128]{2,1,0:T(8,128)S(1)}, u32[]{:S(2)}, u32[]{:S(2)}) %all-to-all-start) | async-done | bytes 524320 | tf_op jit(solution)/shard_map/all_to_all | solution.py:469
  33.9 2.2 %advect.1 = f32[1024,128]{1,0:T(8,128)S(1)} custom-call(f32[1024,128]{1,0:T(8,128)S(1)} %bitcast.8, bf16[512,256]{1,0:T(8,128)(2,1)S(1)} %copy-done, bf16[512,256]{1,0:T(8,128)(2,1)S(1)} %copy-done.1, bf16[256,512]{1,0:T(8,128)(2,1)S(1)} %copy-done.2, bf16[256,512]{1,0:T(8,128)(2,1)S(1)} %copy-done.3, bf16[256,256]{1,0:T(8,128)(2,1)S(1)} %copy-done.5, ...), custom_call_target="tpu_custom_call" | custom-call | tf_op jit(solution)/shard_map/advect/pallas_call | solution.py:458
  36.2 21.0 %all_to_all.10 = f32[64,16,128]{2,1,0:T(8,128)S(1)} all-to-all(f32[64,16,128]{2,1,0:T(8,128)S(1)} %bitcast.9), channel_id=1, replica_groups=mesh['planes'=64,'elem'=4] {'planes'}, dimensions={0} | all-to-all | bytes 1048576 | tf_op jit(solution)/shard_map/all_to_all | solution.py:469
  57.2 0.6 lift.1
  57.8 8.0 %collective-permute-start = (f32[88,128]{1,0:T(8,128)S(1)}, f32[88,128]{1,0:T(8,128)S(1)}, u32[]{:S(2)}, u32[]{:S(2)}) collective-permute-start(f32[88,128]{1,0:T(8,128)S(1)} %get-tuple-element.25), channel_id=1, source_target_pairs={{0,1},{1,2},{2,3},{3,0},{4,5},{5,6},{6,7},{7,4},{8,9},{9,10},{10,1... | collective-permute-start | bytes 135176 | tf_op jit(solution)/shard_map/ppermute | solution.py:473
  65.7 0.4 collective-permute-start.1
  66.2 2.8 %collective-permute-start.2 = (f32[88,128]{1,0:T(8,128)S(1)}, f32[88,128]{1,0:T(8,128)S(1)}, u32[]{:S(2)}, u32[]{:S(2)}) collective-permute-start(f32[88,128]{1,0:T(8,128)S(1)} %get-tuple-element.27), channel_id=1, source_target_pairs={{0,3},{1,0},{2,1},{3,2},{4,7},{5,4},{6,5},{7,6},{8,11},{9,8},{10,9... | collective-permute-start | bytes 135176 | tf_op jit(solution)/shard_map/ppermute | solution.py:473
  69.0 2.4 %collective-permute-done.1.f2_ref = f32[88,128]{1,0:T(8,128)S(1)} collective-permute-done((f32[88,128]{1,0:T(8,128)S(1)}, f32[88,128]{1,0:T(8,128)S(1)}, u32[]{:S(2)}, u32[]{:S(2)}) %collective-permute-start.1) | collective-permute-done | bytes 45088 | tf_op jit(solution)/shard_map/ppermute | solution.py:473
  71.4 2.9 %cg.1 = (f32[64,128]{1,0:T(8,128)S(1)}, f32[64,128]{1,0:T(8,128)S(1)}, f32[64,128]{1,0:T(8,128)S(1)}, f32[64,128]{1,0:T(8,128)S(1)}) custom-call(f32[88,128]{1,0:T(8,128)S(1)} %get-tuple-element.24.f0_ref, f32[88,128]{1,0:T(8,128)S(1)} %collective-permute-done.f1_ref, f32[88,128]{1,0:T(8,128)S(1)} %collective-permute-done.1.f2_ref, ...), custom_call_target="tpu_custom_call" | custom-call | tf_op jit(solution)/shard_map/cg/pallas_call | solution.py:458
  74.3 1.1 %collective-permute-start.3 = (f32[64,128]{1,0:T(8,128)S(1)}, f32[64,128]{1,0:T(8,128)S(1)}, u32[]{:S(2)}, u32[]{:S(2)}) collective-permute-start(f32[64,128]{1,0:T(8,128)S(1)} %get-tuple-element.30), channel_id=1, source_target_pairs={{0,1},{1,2},{2,3},{3,0},{4,5},{5,6},{6,7},{7,4},{8,9},{9,10},{10,1... | collective-permute-start | bytes 98312 | tf_op jit(solution)/shard_map/ppermute | solution.py:473
  75.4 3.0 %collective-permute-start.4 = (f32[64,128]{1,0:T(8,128)S(1)}, f32[64,128]{1,0:T(8,128)S(1)}, u32[]{:S(2)}, u32[]{:S(2)}) collective-permute-start(f32[64,128]{1,0:T(8,128)S(1)} %get-tuple-element.31), channel_id=1, source_target_pairs={{0,2},{1,3},{2,0},{3,1},{4,6},{5,7},{6,4},{7,5},{8,10},{9,11},{10,... | collective-permute-start | bytes 98312 | tf_op jit(solution)/shard_map/ppermute | solution.py:473
  78.4 0.2 collective-permute-start.5
  78.6 1.5 %collective-permute-done.3.t1_ref = f32[64,128]{1,0:T(8,128)S(1)} collective-permute-done((f32[64,128]{1,0:T(8,128)S(1)}, f32[64,128]{1,0:T(8,128)S(1)}, u32[]{:S(2)}, u32[]{:S(2)}) %collective-permute-start.3) | collective-permute-done | bytes 32800 | tf_op jit(solution)/shard_map/ppermute | solution.py:473
  80.1 0.7 collective-permute-done.4.t2_ref
  80.8 1.5 %collective-permute-done.5.t3_ref = f32[64,128]{1,0:T(8,128)S(1)} collective-permute-done((f32[64,128]{1,0:T(8,128)S(1)}, f32[64,128]{1,0:T(8,128)S(1)}, u32[]{:S(2)}, u32[]{:S(2)}) %collective-permute-start.5) | collective-permute-done | bytes 32800 | tf_op jit(solution)/shard_map/ppermute | solution.py:473
  82.3 2.4 %recover.1 = f32[3,4,10368]{2,1,0:T(4,128)} custom-call(f32[64,128]{1,0:T(8,128)S(1)} %get-tuple-element.29.t0_ref, f32[64,128]{1,0:T(8,128)S(1)} %collective-permute-done.3.t1_ref, f32[64,128]{1,0:T(8,128)S(1)} %collective-permute-done.4.t2_ref, f32[64,128]{1,0:T(8,128)S(1)} %collective-permute-done.5.t3_ref, f32[1024,128]{1,0:T(8,128)S(1)} %bitcast.7, ...), custom_call_target="tpu_custom_call" | custom-call | tf_op jit(solution)/shard_map/recover/pallas_call | solution.py:458
  (58 shorter events, 0.2 us)
Async XLA Ops:
  2.4 15.0 %copy-start.26 = (f32[2,81,36]{1,0,2:T(2,128)S(1)}, f32[2,81,36]{1,0,2:T(2,128)}, u32[]{:S(2)}) copy-start(f32[2,81,36]{1,0,2:T(2,128)} %param.29) | copy-start | bytes 69988
  2.4 15.1 %copy-start.11 = (f32[256,81]{1,0:T(8,128)S(1)}, f32[256,81]{1,0:T(8,128)}, u32[]{:S(2)}) copy-start(f32[256,81]{1,0:T(8,128)} %constant.25.clone.node_ref) | copy-start | bytes 248836
  2.4 15.1 %copy-start.12 = (f32[128,256]{1,0:T(8,128)S(1)}, f32[128,256]{1,0:T(8,128)}, u32[]{:S(2)}) copy-start(f32[128,256]{1,0:T(8,128)} %constant.26.clone.mrn_ref) | copy-start | bytes 393220
  2.4 15.1 %copy-start.17 = (f32[128,36]{1,0:T(8,128)S(1)}, f32[128,36]{1,0:T(8,128)}, u32[]{:S(2)}) copy-start(f32[128,36]{1,0:T(8,128)} %constant.24.clone.edge_ref) | copy-start | bytes 55300
  2.4 15.1 %copy-start.18 = (f32[128,128]{1,0:T(8,128)S(1)}, f32[128,128]{1,0:T(8,128)}, u32[]{:S(2)}) copy-start(f32[128,128]{1,0:T(8,128)} %constant.27.clone.mrr_ref) | copy-start | bytes 196612
  2.4 15.1 %copy-start.19 = (f32[128,128]{1,0:T(8,128)S(1)}, f32[128,128]{1,0:T(8,128)}, u32[]{:S(2)}) copy-start(f32[128,128]{1,0:T(8,128)} %constant.28.clone.perm_ref) | copy-start | bytes 196612
  2.4 31.4 %copy-start.5 = (bf16[256,256]{1,0:T(8,128)(2,1)S(1)}, bf16[256,256]{1,0:T(8,128)(2,1)}, u32[]{:S(2)}) copy-start(bf16[256,256]{1,0:T(8,128)(2,1)} %constant.33.clone.ah_ref) | copy-start | bytes 393220
  2.5 31.4 %copy-start.6 = (bf16[256,256]{1,0:T(8,128)(2,1)S(1)}, bf16[256,256]{1,0:T(8,128)(2,1)}, u32[]{:S(2)}) copy-start(bf16[256,256]{1,0:T(8,128)(2,1)} %constant.34.clone.al_ref) | copy-start | bytes 393220
  2.5 31.4 %all-to-all-start = ((f32[64,16,128]{2,1,0:T(8,128)}), f32[64,16,128]{2,1,0:T(8,128)S(1)}, u32[]{:S(2)}, u32[]{:S(2)}) async-start(f32[64,16,128]{2,1,0:T(8,128)} %bitcast.12), calls=%async_computation | async-start | bytes 1048576 | tf_op jit(solution)/shard_map/all_to_all | solution.py:469
  17.3 16.6 %copy-start.3 = (bf16[256,512]{1,0:T(8,128)(2,1)S(1)}, bf16[256,512]{1,0:T(8,128)(2,1)}, u32[]{:S(2)}) copy-start(bf16[256,512]{1,0:T(8,128)(2,1)} %constant.32.clone.dl_ref) | copy-start | bytes 786436
  18.1 15.7 %copy-start = (bf16[512,256]{1,0:T(8,128)(2,1)S(1)}, bf16[512,256]{1,0:T(8,128)(2,1)}, u32[]{:S(2)}) copy-start(bf16[512,256]{1,0:T(8,128)(2,1)} %constant.29.clone.th_ref) | copy-start | bytes 786436
  18.1 15.7 %copy-start.1 = (bf16[512,256]{1,0:T(8,128)(2,1)S(1)}, bf16[512,256]{1,0:T(8,128)(2,1)}, u32[]{:S(2)}) copy-start(bf16[512,256]{1,0:T(8,128)(2,1)} %constant.30.clone.tl_ref) | copy-start | bytes 786436
  18.2 15.7 %copy-start.2 = (bf16[256,512]{1,0:T(8,128)(2,1)S(1)}, bf16[256,512]{1,0:T(8,128)(2,1)}, u32[]{:S(2)}) copy-start(bf16[256,512]{1,0:T(8,128)(2,1)} %constant.31.clone.dh_ref) | copy-start | bytes 786436
  19.7 16.4 %copy-start.7 = (bf16[256,256]{1,0:T(8,128)(2,1)}, bf16[256,256]{1,0:T(8,128)(2,1)S(1)}, u32[]{:S(2)}) copy-start(bf16[256,256]{1,0:T(8,128)(2,1)S(1)} %get-tuple-element.22.lift_low) | copy-start | bytes 393220
  19.7 16.4 %copy-start.9 = (bf16[256,256]{1,0:T(8,128)(2,1)}, bf16[256,256]{1,0:T(8,128)(2,1)S(1)}, u32[]{:S(2)}) copy-start(bf16[256,256]{1,0:T(8,128)(2,1)S(1)} %get-tuple-element.28.w_ref) | copy-start | bytes 393220
  19.7 16.4 %copy-start.13 = (bf16[256,256]{1,0:T(8,128)(2,1)}, bf16[256,256]{1,0:T(8,128)(2,1)S(1)}, u32[]{:S(2)}) copy-start(bf16[256,256]{1,0:T(8,128)(2,1)S(1)} %get-tuple-element.33.rec_high) | copy-start | bytes 393220
  19.7 16.4 %copy-start.15 = (bf16[256,256]{1,0:T(8,128)(2,1)}, bf16[256,256]{1,0:T(8,128)(2,1)S(1)}, u32[]{:S(2)}) copy-start(bf16[256,256]{1,0:T(8,128)(2,1)S(1)} %get-tuple-element.34.rec_low) | copy-start | bytes 393220
  36.1 21.0 %copy-start.8 = (bf16[256,256]{1,0:T(8,128)(2,1)S(1)}, bf16[256,256]{1,0:T(8,128)(2,1)}, u32[]{:S(2)}) copy-start(bf16[256,256]{1,0:T(8,128)(2,1)} %copy-done.7) | copy-start | bytes 393220
  57.8 11.2 %collective-permute-start = (f32[88,128]{1,0:T(8,128)S(1)}, f32[88,128]{1,0:T(8,128)S(1)}, u32[]{:S(2)}, u32[]{:S(2)}) collective-permute-start(f32[88,128]{1,0:T(8,128)S(1)} %get-tuple-element.25), channel_id=1, source_target_pairs={{0,1},{1,2},{2,3},{3,0},{4,5},{5,6},{6,7},{7,4},{8,9},{9,10},{10,1... | collective-permute-start | bytes 135176 | tf_op jit(solution)/shard_map/ppermute | solution.py:473
  65.7 5.6 %collective-permute-start.1 = (f32[88,128]{1,0:T(8,128)S(1)}, f32[88,128]{1,0:T(8,128)S(1)}, u32[]{:S(2)}, u32[]{:S(2)}) collective-permute-start(f32[88,128]{1,0:T(8,128)S(1)} %get-tuple-element.26), channel_id=1, source_target_pairs={{0,2},{1,3},{2,0},{3,1},{4,6},{5,7},{6,4},{7,5},{8,10},{9,11},{10,... | collective-permute-start | bytes 135176 | tf_op jit(solution)/shard_map/ppermute | solution.py:473
  66.2 5.2 %collective-permute-start.2 = (f32[88,128]{1,0:T(8,128)S(1)}, f32[88,128]{1,0:T(8,128)S(1)}, u32[]{:S(2)}, u32[]{:S(2)}) collective-permute-start(f32[88,128]{1,0:T(8,128)S(1)} %get-tuple-element.27), channel_id=1, source_target_pairs={{0,3},{1,0},{2,1},{3,2},{4,7},{5,4},{6,5},{7,6},{8,11},{9,8},{10,9... | collective-permute-start | bytes 135176 | tf_op jit(solution)/shard_map/ppermute | solution.py:473
  74.3 5.8 %collective-permute-start.3 = (f32[64,128]{1,0:T(8,128)S(1)}, f32[64,128]{1,0:T(8,128)S(1)}, u32[]{:S(2)}, u32[]{:S(2)}) collective-permute-start(f32[64,128]{1,0:T(8,128)S(1)} %get-tuple-element.30), channel_id=1, source_target_pairs={{0,1},{1,2},{2,3},{3,0},{4,5},{5,6},{6,7},{7,4},{8,9},{9,10},{10,1... | collective-permute-start | bytes 98312 | tf_op jit(solution)/shard_map/ppermute | solution.py:473
  75.4 5.4 %collective-permute-start.4 = (f32[64,128]{1,0:T(8,128)S(1)}, f32[64,128]{1,0:T(8,128)S(1)}, u32[]{:S(2)}, u32[]{:S(2)}) collective-permute-start(f32[64,128]{1,0:T(8,128)S(1)} %get-tuple-element.31), channel_id=1, source_target_pairs={{0,2},{1,3},{2,0},{3,1},{4,6},{5,7},{6,4},{7,5},{8,10},{9,11},{10,... | collective-permute-start | bytes 98312 | tf_op jit(solution)/shard_map/ppermute | solution.py:473
  78.4 3.9 %collective-permute-start.5 = (f32[64,128]{1,0:T(8,128)S(1)}, f32[64,128]{1,0:T(8,128)S(1)}, u32[]{:S(2)}, u32[]{:S(2)}) collective-permute-start(f32[64,128]{1,0:T(8,128)S(1)} %get-tuple-element.32), channel_id=1, source_target_pairs={{0,3},{1,0},{2,1},{3,2},{4,7},{5,4},{6,5},{7,6},{8,11},{9,8},{10,9... | collective-permute-start | bytes 98312 | tf_op jit(solution)/shard_map/ppermute | solution.py:473
  (11 other events, 112.6 us)
